TPU v7x, 32 devices: a whole 2x2x4 slice. The times are simulated.
32 devices in a mesh: gx: 4 (over z), gy: 4 (over y, core), gz: 2 (over x).
Axes of the slice: x: 2, y: 2, z: 4, core: 2. Of those that a mesh axis runs over, the one named last changes fastest.
Arguments:
- volume: bfloat16 [32, 64, 32, 128], P('gx', 'gy', 'gz'), may hold values from -6 to 6
- w_full: bfloat16 [3, 3, 3, 128, 128], replicated, may hold values from -0.15625 to 0.15625
- w_half: bfloat16 [3, 3, 3, 128, 256], replicated, may hold values from -0.15625 to 0.15625
- w_bottom_in: bfloat16 [3, 3, 3, 256, 512], P(None, None, None, None, 'gx'), may hold values from -0.109375 to 0.109375
- w_bottom_out: bfloat16 [3, 3, 3, 512, 512], P(None, None, None, None, 'gx'), may hold values from -0.078125 to 0.078125
- w_up: bfloat16 [3, 3, 3, 768, 256], replicated, may hold values from -0.0625 to 0.0625
Outputs:
- decoded: bfloat16 [16, 32, 16, 256], P('gx', 'gy', 'gz')
All inputs are finite; a program needn't handle non-finite values.
Results may differ from a plain program's by a relative error of at most 0.009.
Values may be sent and summed in bfloat16 or wider, within the bound.
A program may use at most 64 MiB of HBM per device.

v0:
```python
import functools

import jax
import jax.numpy as jnp
from jax import lax
from jax.experimental import pallas as pl
from jax.experimental.pallas import tpu as pltpu
from jax.sharding import PartitionSpec as P

F32 = jnp.float32
BF16 = jnp.bfloat16
STEPS = [(dx, dy) for dx in (-1, 0, 1) for dy in (-1, 0, 1)]


def span(d, n, pad):
    if d == 0:
        return pl.ds(pad, n), pl.ds(1, n)
    if d < 0:
        return pl.ds(pad, 1), pl.ds(n + 1, 1)
    return pl.ds(pad + n - 1, 1), pl.ds(0, 1)


def kernel(
    dims,
    v, wf_h, wh_h, w1_h, w2_h, wu_h,
    out,
    wf, wh, w1, w2, wu, wsem, wt,
    p1, f1, g1, e1, t1,
    p2, f2, g2, e2,
    p3, f3, g3, e3, acc,
    pk2, l2, sel2, q2, pk3, l3, q3, pk4, l4, vup,
    s1, r1, s2, r2, s3, r3, s4, r4, s5, r5, s6, r6,
):
    gxn, gyn = dims
    gx, gy, gz = lax.axis_index("gx"), lax.axis_index("gy"), lax.axis_index("gz")
    oz = 1 - gz

    loads = [
        pltpu.make_async_copy(src, dst, wsem.at[i])
        for i, (src, dst) in enumerate(((wf_h, wf), (wh_h, wh), (w1_h, w1), (w2_h, w2), (wu_h, wu)))
    ]
    for load in loads:
        load.start()

    def on(cond, fn):
        if cond is True:
            fn()
        else:
            pl.when(cond)(fn)

    def exists(dx, dy):
        conds = []
        if dx < 0:
            conds.append(gx > 0)
        if dx > 0:
            conds.append(gx < gxn - 1)
        if dy < 0:
            conds.append(gy > 0)
        if dy > 0:
            conds.append(gy < gyn - 1)
        if not conds:
            return True
        return functools.reduce(jnp.logical_and, conds)

    for ref in (p1, g1, p2, g2, p3, g3, l2, l3, l4):
        ref[...] = jnp.zeros(ref.shape, ref.dtype)

    barrier = pltpu.get_barrier_semaphore()
    for s in range(gxn):
        there = lax.rem(gx + s, gxn)
        for dy in (-1, 0, 1):
            for z in (0, 1):
                if s == 0 and dy == 0 and z == 0:
                    continue

                def signal(there=there, dy=dy, z=z):
                    pl.semaphore_signal(
                        barrier, inc=1,
                        device_id={"gx": there, "gy": gy + dy, "gz": oz if z else gz},
                        device_id_type=pl.DeviceIdType.MESH,
                    )

                on(exists(0, dy), signal)
    lines = 1 + (gy > 0).astype(jnp.int32) + (gy < gyn - 1).astype(jnp.int32)
    pl.semaphore_wait(barrier, 2 * gxn * lines - 1)

    def send(src, dst, ss, rs, x, y, z):
        return pltpu.make_async_remote_copy(
            src_ref=src, dst_ref=dst, send_sem=ss, recv_sem=rs,
            device_id={"gx": x, "gy": y, "gz": z}, device_id_type=pl.DeviceIdType.MESH,
        )

    late = []

    def neighbours(src, pad, face, rim, side, nx, ny, ss, rs):
        arrivals = []
        for i, (dx, dy) in enumerate(STEPS):
            sx, tx = span(dx, nx, pad)
            sy, ty = span(dy, ny, pad)
            fx, _ = span(dx, nx, 0)
            fy, _ = span(dy, ny, 0)
            copies = [send(face.at[fx, fy], side.at[tx, ty], ss.at[9 + i], rs.at[9 + i], gx + dx, gy + dy, oz)]
            if (dx, dy) != (0, 0):
                copies.append(send(src.at[sx, sy], rim.at[tx, ty], ss.at[i], rs.at[i], gx + dx, gy + dy, gz))
            for copy in copies:
                on(exists(dx, dy), copy.start)
                late.append((exists(dx, dy), copy.wait_send))
                arrivals.append((exists(-dx, -dy), copy.wait_recv))

        def wait():
            for cond, fn in arrivals:
                on(cond, fn)

        return wait

    def edge(block):
        size = block.shape[-2]
        rows = lax.broadcasted_iota(jnp.int32, block.shape, block.ndim - 2)
        return jnp.sum(jnp.where(rows == (size - 1) * oz, block, 0.0), axis=block.ndim - 2, keepdims=True)

    def shifted(block, fill):
        size = block.shape[-2]
        axis = block.ndim - 2
        rows = lax.broadcasted_iota(jnp.int32, block.shape, axis)
        below = jnp.where(rows == 0, 0.0, pltpu.roll(block, 1, axis))
        above = jnp.where(rows == size - 1, 0.0, pltpu.roll(block, size - 1, axis))
        if fill is not None:
            fill = jnp.broadcast_to(fill, block.shape)
            below = jnp.where(rows == jnp.where(gz == 1, 0, -1), fill, below)
            above = jnp.where(rows == jnp.where(gz == 0, size - 1, -1), fill, above)
        return below, above

    def rounded(x):
        return x.astype(BF16).astype(F32)

    nx, ny, nz, c0 = v.shape
    for x in range(nx):
        f1[x] = edge(v[x].astype(F32))
    arrived = neighbours(v, 0, f1, p1, g1, nx, ny, s1, r1)
    p1[1 : nx + 1, 1 : ny + 1] = v[...]

    loads[0].wait()
    k0 = 3 * c0
    for oy in range(3):
        for plane in range(4):
            at = pl.ds(plane * k0, k0)
            wt[oy, at, :c0] = wf[plane * 3 + oy] if plane < 3 else jnp.zeros((k0, c0), BF16)
            wt[oy, at, c0:] = wf[(plane - 1) * 3 + oy] if plane > 0 else jnp.zeros((k0, c0), BF16)
    arrived()

    @pl.loop(0, nx + 2)
    def _(x):
        block = p1[x].astype(F32)
        below, above = shifted(block, g1[x])
        e1[x, :, :, 0:c0] = below.astype(BF16)
        e1[x, :, :, c0 : 2 * c0] = p1[x]
        e1[x, :, :, 2 * c0 :] = above.astype(BF16)

    def full_rows(x):
        total = jnp.zeros((ny * nz, 2 * c0), F32)
        for oy in range(3):
            for half in range(2):
                lhs = [e1[x + 2 * half + i, oy : oy + ny].reshape(ny * nz, k0) for i in range(2)]
                rhs = wt[oy, 2 * half * k0 : 2 * (half + 1) * k0]
                total = total + jnp.dot(jnp.concatenate(lhs, axis=1), rhs, preferred_element_type=F32)
        return jnp.maximum(jnp.maximum(total[:, :c0], total[:, c0:]), 0.0)

    hx, hy, hz = nx // 2, ny // 2, nz // 2

    @pl.loop(0, hx)
    def _(x):
        both = full_rows(2 * x).reshape(hy, 2, nz, c0)
        t1[...] = jnp.max(both, axis=1)
        small = jnp.maximum(t1[:, pl.ds(0, hz, stride=2), :], t1[:, pl.ds(1, hz, stride=2), :])
        small = rounded(small)
        p2[x + 1, 1 : hy + 1] = small
        f2[x] = edge(small)

    arrived = neighbours(p2, 1, f2, p2, g2, hx, hy, s2, r2)
    arrived()
    for x in range(hx + 2):
        block = p2[x]
        below, above = shifted(block, g2[x])
        e2[0, x], e2[1, x], e2[2, x] = below, block, above
    loads[1].wait()
    rows = hx * hy * hz
    c1 = wh.shape[2]
    total = jnp.zeros((rows, c1), F32)
    for ox in range(3):
        for oy in range(3):
            for k in range(3):
                lhs = e2[k, ox : ox + hx, oy : oy + hy].reshape(rows, c0).astype(BF16)
                total = total + jnp.dot(lhs, wh[(ox * 3 + oy) * 3 + k], preferred_element_type=F32)
    skip = rounded(jnp.maximum(total, 0.0)).reshape(hx, hy, hz, c1)
    p3[1 : hx + 1, 1 : hy + 1] = skip
    f3[...] = edge(skip)

    cx, cy, cz = hx // 2, hy // 2, hz // 2
    ax = gxn * cx
    group = cz * cx
    m = jnp.max(skip.reshape(cx, 2, cy, 2, hz, c1), axis=(1, 3))
    m = m.reshape(cx * cy * hz, c1)
    m = jnp.maximum(m, pltpu.roll(m, m.shape[0] - 1, 0)).astype(BF16)

    blocks = []
    lane = lax.broadcasted_iota(jnp.int32, (group, cx * cy * hz), 1)
    sub = lax.broadcasted_iota(jnp.int32, (group, cx * cy * hz), 0)
    shift_x = cx.bit_length() - 1
    sub_x = sub & (cx - 1)
    sub_o = sub >> shift_x
    for y in range(cy):
        blocks.append(jnp.where(lane == (sub_x * cy + y) * hz + 2 * sub_o, 1.0, 0.0))
    blocks.append(jnp.where(lane == (sub_x * cy + sub_o) * hz + 2 * (cz - 1) * oz, 1.0, 0.0))
    pick = jnp.concatenate(blocks, axis=0).astype(BF16)
    packets = jnp.dot(pick, m, preferred_element_type=F32).reshape(cy + 1, group, c1).astype(BF16)
    pk2[...] = packets
    l2[gx, 0:cy] = packets[0:cy]

    slots = cy + 5

    def coarse_copy(s, dy, z, k):
        def make(src_gx, tgt_gx):
            if z == 0:
                src = {0: pl.ds(0, cy), -1: pl.ds(0, 1), 1: pl.ds(cy - 1, 1)}[dy]
                dst = {0: pl.ds(0, cy), 1: pl.ds(cy, 1), -1: pl.ds(cy + 1, 1)}[dy]
            else:
                src = pl.ds(cy, 1)
                dst = {0: pl.ds(cy + 2, 1), 1: pl.ds(cy + 3, 1), -1: pl.ds(cy + 4, 1)}[dy]
            return send(pk2.at[src], l2.at[src_gx, dst], s4.at[s, k], r4.at[s, k], tgt_gx, gy + dy, oz if z else gz)

        return make

    def deep_copy(pk, land, ss, rs):
        def choose(s, dy, z, k):
            def make(src_gx, tgt_gx):
                sy, ty = span(dy, cy, 0)
                sender = gz if src_gx is gx else (oz if z else gz)
                if z == 0:
                    src = pk.at[sy]
                    dst = land.at[src_gx, ty, pl.ds(1, cz)]
                else:
                    src = pk.at[sy, pl.ds((cz - 1) * (1 - sender), 1)]
                    dst = land.at[src_gx, ty, pl.ds((cz + 1) * sender, 1)]
                return send(src, dst, ss.at[s, k], rs.at[s, k], tgt_gx, gy + dy, oz if z else gz)

            return make

        return choose

    def narrow_copy(s, dy, z, k):
        def make(src_gx, tgt_gx):
            sy, ty = span(dy, cy, 0)
            sender = gz if src_gx is gx else (oz if z else gz)
            if z == 0:
                src = pk4.at[tgt_gx, sy]
                dst = l4.at[src_gx, ty, pl.ds(1, cz // 2)]
            else:
                src = pk4.at[tgt_gx, sy, pl.ds((cz // 2 - 1) * (1 - sender), 1)]
                dst = l4.at[src_gx, ty, pl.ds((cz // 2 + 1) * sender, 1)]
            return send(src, dst, s6.at[s, k], r6.at[s, k], tgt_gx, gy + dy, oz if z else gz)

        return make

    def column_exchange(choose):
        arrivals = []
        for s in list(range(1, gxn)) + [0]:
            there = lax.rem(gx + s, gxn)
            origin = lax.rem(gx + gxn - s, gxn)
            for k, (dy, z) in enumerate(((0, 0), (-1, 0), (1, 0), (0, 1), (-1, 1), (1, 1))):
                if s == 0 and k == 0:
                    continue
                make = choose(s, dy, z, k)
                copy = make(gx, there)
                on(exists(0, dy), copy.start)
                late.append((exists(0, dy), copy.wait_send))
                arrivals.append((exists(0, -dy), make(origin, there).wait_recv))

        def wait():
            for cond, fn in arrivals:
                on(cond, fn)

        return wait

    arrived = column_exchange(coarse_copy)

    span_g = slots * group
    width = gxn * span_g
    lane = lax.broadcasted_iota(jnp.int32, (ax, width), 1)
    xs = lax.broadcasted_iota(jnp.int32, (ax, width), 0)
    base = lane - ((xs >> shift_x) * span_g + (xs & (cx - 1)))
    for y in range(-1, cy + 1):
        for z in range(-1, cz + 1):
            if 0 <= z < cz:
                slot = y if 0 <= y < cy else (cy if y < 0 else cy + 1)
                at = slot * group + z * cx
            else:
                slot = cy + 2 if 0 <= y < cy else (cy + 3 if y < 0 else cy + 4)
                line = y if 0 <= y < cy else (cy - 1 if y < 0 else 0)
                mine = (gz == 1) if z < 0 else (gz == 0)
                at = jnp.where(mine, slot * group + line * cx, -width * 4)
            sel2[y + 1, z + 1] = jnp.where(base == at, 1.0, 0.0)

    rim = (cy + 2) * (cz + 2) * ax
    select = sel2[...].reshape(rim, width).astype(BF16)
    arrived()
    skip_arrived = neighbours(p3, 1, f3, p3, g3, hx, hy, s3, r3)
    landed = l2[...].astype(F32).reshape(width, c1).astype(BF16)
    block = jnp.dot(select, landed, preferred_element_type=F32).reshape(cy + 2, cz + 2, ax, c1)

    def spread(q, block):
        below, above = shifted(block, None)
        q[0], q[1], q[2] = below, block, above

    deep = cy * cz * ax
    fo = w1.shape[2]

    def bottom(q, w):
        total = jnp.zeros((deep, fo), F32)
        for ox in range(3):
            for oy in range(3):
                for k in range(3):
                    lhs = q[ox, oy : oy + cy, k : k + cz].reshape(deep, q.shape[-1]).astype(BF16)
                    total = total + jnp.dot(lhs, w[(ox * 3 + oy) * 3 + k], preferred_element_type=F32)
        return jnp.maximum(total, 0.0).reshape(cy, cz, ax, fo).astype(BF16)

    spread(q2, block)
    loads[2].wait()
    first = bottom(q2, w1)
    pk3[...] = first
    l3[gx, 1 : cy + 1, 1 : cz + 1] = first
    arrived = column_exchange(deep_copy(pk3, l3, s5, r5))

    skip_arrived()
    for x in range(hx + 2):
        block = p3[x]
        below, above = shifted(block, g3[x])
        e3[0, x], e3[1, x], e3[2, x] = below, block, above
    loads[4].wait()
    c2 = w2.shape[1]
    total = jnp.zeros((rows, c1), F32)
    for ox in range(3):
        for oy in range(3):
            for k in range(3):
                lhs = e3[k, ox : ox + hx, oy : oy + hy].reshape(rows, c1).astype(BF16)
                total = total + jnp.dot(lhs, wu[(ox * 3 + oy) * 3 + k, c2:, :], preferred_element_type=F32)
    acc[...] = total.reshape(hx, hy, hz, c1)

    near = cx + 2
    wide = gxn * cz * near
    lane = lax.broadcasted_iota(jnp.int32, (wide, cz * ax), 1)
    row = lax.broadcasted_iota(jnp.int32, (wide, cz * ax), 0)
    shift_n = near.bit_length() - 1
    shift_z = cz.bit_length() - 1
    at = (row >> (shift_n + shift_z)) * cx + (row & (near - 1)) - 1
    at = jnp.where(jnp.logical_and(at >= 0, at < ax), at, -(cz + 1) * ax)
    share = jnp.where(lane == ((row >> shift_n) & (cz - 1)) * ax + at, 1.0, 0.0).astype(BF16)

    lane = lax.broadcasted_iota(jnp.int32, (hz, (cz + 4) * near), 1)
    zs = lax.broadcasted_iota(jnp.int32, (hz, (cz + 4) * near), 0)
    blocks = []
    for k in range(3):
        for x in range(-1, hx + 1):
            blocks.append(jnp.where(lane == (((zs + (k - 1)) >> 1) + 2) * near + (x >> 1) + 1, 1.0, 0.0))
    pick = jnp.concatenate(blocks, axis=0).astype(BF16)

    arrived()
    spread(q3, jnp.concatenate([l3[g].astype(F32) for g in range(gxn)], axis=-1))
    loads[3].wait()
    second = bottom(q3, w2)
    for y in range(cy):
        line = second[y].astype(F32).reshape(cz * ax, fo).astype(BF16)
        line = jnp.dot(share, line, preferred_element_type=F32)
        pk4[:, y] = line.reshape(gxn, cz // 2, 2 * near, fo).astype(BF16)
    l4[gx, 1 : cy + 1, 1 : cz // 2 + 1] = pk4[gx]
    arrived = column_exchange(narrow_copy)
    arrived()
    for y in range(cy + 2):
        field = jnp.concatenate([l4[g, y].astype(F32) for g in range(gxn)], axis=-1)
        field = field.reshape((cz + 4) * near, c2).astype(BF16)
        vup[:, y] = jnp.dot(pick, field, preferred_element_type=F32).reshape(3, hx + 2, hz, c2)

    parts = []
    for oy in range(3):
        low, high = (oy + 1) // 2, (hy - 1 + oy + 1) // 2 + 1
        count = high - low
        total = jnp.zeros((count * hx * hz, c1), F32)
        for ox in range(3):
            for k in range(3):
                lhs = vup[k, low:high, ox : ox + hx].reshape(count * hx * hz, c2).astype(BF16)
                total = total + jnp.dot(lhs, wu[(ox * 3 + oy) * 3 + k, :c2, :], preferred_element_type=F32)
        parts.append((low, total.reshape(count, hx, hz, c1)))
    for y in range(hy):
        line = acc[:, y]
        for oy in range(3):
            low, part = parts[oy]
            line = line + part[(y + oy + 1) // 2 - low]
        out[:, y] = line.astype(BF16)

    for cond, fn in late:
        on(cond, fn)


def on_device(dims, volume, w_full, w_half, w_bottom_in, w_bottom_out, w_up):
    gxn, gyn = dims
    nx, ny, nz, c0 = volume.shape
    c1 = w_half.shape[4]
    c2, fo = w_bottom_out.shape[3:]
    hx, hy, hz = nx // 2, ny // 2, nz // 2
    cx, cy, cz = hx // 2, hy // 2, hz // 2
    ax = gxn * cx
    weights = [
        w_full.reshape(9, 3 * c0, c0),
        w_half.reshape(27, c0, c1),
        w_bottom_in.reshape(27, c1, fo),
        w_bottom_out.reshape(27, c2, fo),
        w_up.reshape(27, c2 + c1, c1),
    ]
    vm = pltpu.VMEM
    dma = pltpu.SemaphoreType.DMA
    scratch = [vm(w.shape, BF16) for w in weights] + [dma((5,)), vm((3, 12 * c0, 2 * c0), BF16)]
    scratch += [
        vm((nx + 2, ny + 2, nz, c0), BF16), vm((nx, ny, 1, c0), F32), vm((nx + 2, ny + 2, 1, c0), F32),
        vm((nx + 2, ny + 2, nz, 3 * c0), BF16), vm((hy, nz, c0), F32),
        vm((hx + 2, hy + 2, hz, c0), F32), vm((hx, hy, 1, c0), F32), vm((hx + 2, hy + 2, 1, c0), F32),
        vm((3, hx + 2, hy + 2, hz, c0), F32),
        vm((hx + 2, hy + 2, hz, c1), F32), vm((hx, hy, 1, c1), F32), vm((hx + 2, hy + 2, 1, c1), F32),
        vm((3, hx + 2, hy + 2, hz, c1), F32), vm((hx, hy, hz, c1), F32),
        vm((cy + 1, cz * cx, c1), BF16), vm((gxn, cy + 5, cz * cx, c1), BF16),
        vm((cy + 2, cz + 2, ax, gxn * (cy + 5) * cz * cx), F32), vm((3, cy + 2, cz + 2, ax, c1), F32),
        vm((cy, cz, ax, fo), BF16), vm((gxn, cy + 2, cz + 2, ax, fo), BF16), vm((3, cy + 2, cz + 2, ax, c2), F32),
        vm((gxn, cy, cz // 2, 2 * (cx + 2), fo), BF16), vm((gxn, cy + 2, cz // 2 + 2, 2 * (cx + 2), fo), BF16),
        vm((3, cy + 2, hx + 2, hz, c2), F32),
    ]
    scratch += [dma((18,))] * 6 + [dma((gxn, 6))] * 6
    return pl.pallas_call(
        functools.partial(kernel, dims),
        out_shape=jax.ShapeDtypeStruct((hx, hy, hz, c1), BF16),
        in_specs=[pl.BlockSpec(memory_space=pltpu.VMEM)] + [pl.BlockSpec(memory_space=pl.ANY)] * 5,
        out_specs=pl.BlockSpec(memory_space=pltpu.VMEM),
        scratch_shapes=scratch,
        compiler_params=pltpu.CompilerParams(
            collective_id=0, has_side_effects=True, vmem_limit_bytes=60 * 1024 * 1024
        ),
    )(volume, *weights)


def solution(mesh):
    dims = (mesh.shape["gx"], mesh.shape["gy"])
    assert mesh.shape["gz"] == 2
    return jax.shard_map(
        functools.partial(on_device, dims),
        mesh=mesh,
        in_specs=(
            P("gx", "gy", "gz", None),
            P(),
            P(),
            P(None, None, None, None, "gx"),
            P(None, None, None, None, "gx"),
            P(),
        ),
        out_specs=P("gx", "gy", "gz", None),
        check_vma=False,
    )
```

profile of v0, /device:TPU:0, one launch (start us, length us, event | category | flops | bytes accessed | tf_op | source)
XLA Modules:
  0.0 49.1 jit_solution(14770528035685618952)
XLA Ops:
  0.0 47.5 %shard_map.64 = bf16[4,8,8,256]{3,2,1,0:T(8,128)(2,1)} custom-call(bf16[8,16,16,128]{3,2,1,0:T(8,128)(2,1)} %v.1, bf16[9,384,128]{2,1,0:T(8,128)(2,1)} %bitcast.9, bf16[27,128,256]{2,1,0:T(8,128)(2,1)} %bitcast.7, bf16[27,256,128]{2,1,0:T(8,128)(2,1)} %bitcast.8, bf16[27,512,128]{2,1,0:T(8,128)(2,1)} %bitcast.6, bf16[27,768,256]{2,1,0:T(8,128)(2,1)} %bitcast.5), custom_call_target="tpu_custom_call" | custom-call | tf_op jit(solution)/shard_map/pallas_call | solution.py:435
  47.5 1.6 %copy.8 = bf16[4,8,8,256]{3,2,1,0:T(8,128)(2,1)} copy(bf16[4,8,8,256]{3,2,1,0:T(8,128)(2,1)} %shard_map.64) | data formatting | bytes 262144
where the time goes:
time: 49.4 us; the launch traced here: 49.1 us
  Pallas kernels  47.5 us (96%)
  local copies, waits for them, and re-layouts  1.57 us (3%)
    pallas_call x1, Pallas kernels, on_device(): pl.pallas_call(functools.partial(kernel, dims), out_shape=jax.ShapeDtypeS...  47.5 us
    unnamed x1, local copies, waits for them, and re-layouts  1.57 us

commit v1 on v0

--- a/solution.py
+++ b/solution.py
@@ -90,28 +90,48 @@
             device_id={"gx": x, "gy": y, "gz": z}, device_id_type=pl.DeviceIdType.MESH,
         )
 
+    many_x = jnp.logical_and(gx > 0, gx < gxn - 1)
+    many_y = jnp.logical_and(gy > 0, gy < gyn - 1)
+
+    def by_y(fn):
+        for b in (1, 2):
+            pl.when(many_y if b == 2 else jnp.logical_not(many_y))(functools.partial(fn, b))
+
+    def by_xy(fn):
+        for a in (1, 2):
+            for b in (1, 2):
+                cx_ = many_x if a == 2 else jnp.logical_not(many_x)
+                cy_ = many_y if b == 2 else jnp.logical_not(many_y)
+                pl.when(jnp.logical_and(cx_, cy_))(functools.partial(fn, a, b))
+
+    def drain(ref, sem):
+        pltpu.make_async_copy(ref, ref, sem).wait()
+
     late = []
 
     def neighbours(src, pad, face, rim, side, nx, ny, ss, rs):
-        arrivals = []
-        for i, (dx, dy) in enumerate(STEPS):
+        for dx, dy in STEPS:
             sx, tx = span(dx, nx, pad)
             sy, ty = span(dy, ny, pad)
             fx, _ = span(dx, nx, 0)
             fy, _ = span(dy, ny, 0)
-            copies = [send(face.at[fx, fy], side.at[tx, ty], ss.at[9 + i], rs.at[9 + i], gx + dx, gy + dy, oz)]
+            copies = [send(face.at[fx, fy], side.at[tx, ty], ss.at[0], rs.at[0], gx + dx, gy + dy, oz)]
             if (dx, dy) != (0, 0):
-                copies.append(send(src.at[sx, sy], rim.at[tx, ty], ss.at[i], rs.at[i], gx + dx, gy + dy, gz))
+                k = 1 if dx else 2
+                copies.append(send(src.at[sx, sy], rim.at[tx, ty], ss.at[k], rs.at[k], gx + dx, gy + dy, gz))
             for copy in copies:
                 on(exists(dx, dy), copy.start)
-                late.append((exists(dx, dy), copy.wait_send))
-                arrivals.append((exists(-dx, -dy), copy.wait_recv))
-
-        def wait():
-            for cond, fn in arrivals:
-                on(cond, fn)
-
-        return wait
+
+        def finish(sems):
+            def both(a, b):
+                drain(side.at[0 : nx + a, 0 : ny + b], sems.at[0])
+                drain(rim.at[0:a, 0 : ny + b], sems.at[1])
+                drain(rim.at[0:nx, 0:b], sems.at[2])
+
+            by_xy(both)
+
+        late.append(lambda: finish(ss))
+        return lambda: finish(rs)
 
     def edge(block):
         size = block.shape[-2]
@@ -218,7 +238,7 @@
 
     slots = cy + 5
 
-    def coarse_copy(s, dy, z, k):
+    def coarse_copy(k, dy, z):
         def make(src_gx, tgt_gx):
             if z == 0:
                 src = {0: pl.ds(0, cy), -1: pl.ds(0, 1), 1: pl.ds(cy - 1, 1)}[dy]
@@ -226,12 +246,12 @@
             else:
                 src = pl.ds(cy, 1)
                 dst = {0: pl.ds(cy + 2, 1), 1: pl.ds(cy + 3, 1), -1: pl.ds(cy + 4, 1)}[dy]
-            return send(pk2.at[src], l2.at[src_gx, dst], s4.at[s, k], r4.at[s, k], tgt_gx, gy + dy, oz if z else gz)
+            return send(pk2.at[src], l2.at[src_gx, dst], s4.at[k], r4.at[k], tgt_gx, gy + dy, oz if z else gz)
 
         return make
 
     def deep_copy(pk, land, ss, rs):
-        def choose(s, dy, z, k):
+        def choose(k, dy, z):
             def make(src_gx, tgt_gx):
                 sy, ty = span(dy, cy, 0)
                 sender = gz if src_gx is gx else (oz if z else gz)
@@ -241,13 +261,13 @@
                 else:
                     src = pk.at[sy, pl.ds((cz - 1) * (1 - sender), 1)]
                     dst = land.at[src_gx, ty, pl.ds((cz + 1) * sender, 1)]
-                return send(src, dst, ss.at[s, k], rs.at[s, k], tgt_gx, gy + dy, oz if z else gz)
+                return send(src, dst, ss.at[k], rs.at[k], tgt_gx, gy + dy, oz if z else gz)
 
             return make
 
         return choose
 
-    def narrow_copy(s, dy, z, k):
+    def narrow_copy(k, dy, z):
         def make(src_gx, tgt_gx):
             sy, ty = span(dy, cy, 0)
             sender = gz if src_gx is gx else (oz if z else gz)
@@ -257,31 +277,45 @@
             else:
                 src = pk4.at[tgt_gx, sy, pl.ds((cz // 2 - 1) * (1 - sender), 1)]
                 dst = l4.at[src_gx, ty, pl.ds((cz // 2 + 1) * sender, 1)]
-            return send(src, dst, s6.at[s, k], r6.at[s, k], tgt_gx, gy + dy, oz if z else gz)
+            return send(src, dst, s6.at[k], r6.at[k], tgt_gx, gy + dy, oz if z else gz)
 
         return make
 
-    def column_exchange(choose):
-        arrivals = []
+    def column_exchange(choose, away, home):
         for s in list(range(1, gxn)) + [0]:
             there = lax.rem(gx + s, gxn)
-            origin = lax.rem(gx + gxn - s, gxn)
             for k, (dy, z) in enumerate(((0, 0), (-1, 0), (1, 0), (0, 1), (-1, 1), (1, 1))):
                 if s == 0 and k == 0:
                     continue
-                make = choose(s, dy, z, k)
-                copy = make(gx, there)
-                on(exists(0, dy), copy.start)
-                late.append((exists(0, dy), copy.wait_send))
-                arrivals.append((exists(0, -dy), make(origin, there).wait_recv))
-
-        def wait():
-            for cond, fn in arrivals:
-                on(cond, fn)
-
-        return wait
-
-    arrived = column_exchange(coarse_copy)
+                on(exists(0, dy), choose(0 if s else 1 + z, dy, z)(gx, there).start)
+
+        def finish(which):
+            def both(b):
+                drain(*away(b, which))
+                for k in (0, 1):
+                    drain(*home(b, k, which))
+
+            by_y(both)
+
+        late.append(lambda: finish(0))
+        return lambda: finish(1)
+
+    def blocks_of(land, sems):
+        wz = land.shape[2] - 2
+
+        def away(b, which):
+            return land.at[0 : gxn - 1, 0 : cy + b, 0 : wz + 1], sems[which].at[0]
+
+        def home(b, k, which):
+            return land.at[0, 0 : (cy if k else 0) + b, 0 : 1 if k else wz], sems[which].at[1 + k]
+
+        return away, home
+
+    arrived = column_exchange(
+        coarse_copy,
+        lambda b, which: (l2.at[0 : gxn - 1, 0 : cy + 1 + 2 * b], (s4, r4)[which].at[0]),
+        lambda b, k, which: (l2.at[0, 0 : b + k], (s4, r4)[which].at[1 + k]),
+    )
 
     span_g = slots * group
     width = gxn * span_g
@@ -328,7 +362,7 @@
     first = bottom(q2, w1)
     pk3[...] = first
     l3[gx, 1 : cy + 1, 1 : cz + 1] = first
-    arrived = column_exchange(deep_copy(pk3, l3, s5, r5))
+    arrived = column_exchange(deep_copy(pk3, l3, s5, r5), *blocks_of(l3, (s5, r5)))
 
     skip_arrived()
     for x in range(hx + 2):
@@ -372,7 +406,7 @@
         line = jnp.dot(share, line, preferred_element_type=F32)
         pk4[:, y] = line.reshape(gxn, cz // 2, 2 * near, fo).astype(BF16)
     l4[gx, 1 : cy + 1, 1 : cz // 2 + 1] = pk4[gx]
-    arrived = column_exchange(narrow_copy)
+    arrived = column_exchange(narrow_copy, *blocks_of(l4, (s6, r6)))
     arrived()
     for y in range(cy + 2):
         field = jnp.concatenate([l4[g, y].astype(F32) for g in range(gxn)], axis=-1)
@@ -396,8 +430,8 @@
             line = line + part[(y + oy + 1) // 2 - low]
         out[:, y] = line.astype(BF16)
 
-    for cond, fn in late:
-        on(cond, fn)
+    for fn in late:
+        fn()
 
 
 def on_device(dims, volume, w_full, w_half, w_bottom_in, w_bottom_out, w_up):
@@ -431,7 +465,7 @@
         vm((gxn, cy, cz // 2, 2 * (cx + 2), fo), BF16), vm((gxn, cy + 2, cz // 2 + 2, 2 * (cx + 2), fo), BF16),
         vm((3, cy + 2, hx + 2, hz, c2), F32),
     ]
-    scratch += [dma((18,))] * 6 + [dma((gxn, 6))] * 6
+    scratch += [dma((3,))] * 12
     return pl.pallas_call(
         functools.partial(kernel, dims),
         out_shape=jax.ShapeDtypeStruct((hx, hy, hz, c1), BF16),

time: 49.4 us -> 47.3 us (0.957)
  Pallas kernels: 47.5 us -> 45.5 us
    pallas_call x1, Pallas kernels: 47.5 us -> 45.5 us  [on_device(): pl.pallas_call(functools.partial(kernel, dims), out_shape=jax.ShapeDtypeS...]
where the time goes in v1:
time: 47.3 us; the launch traced here: 47 us
  Pallas kernels  45.5 us (96%)
  local copies, waits for them, and re-layouts  1.57 us (3%)
    pallas_call x1, Pallas kernels, on_device(): pl.pallas_call(functools.partial(kernel, dims), out_shape=jax.ShapeDtypeS...  45.5 us
    unnamed x1, local copies, waits for them, and re-layouts  1.57 us

profile of v1, /device:TPU:0, one launch (start us, length us, event | category | flops | bytes accessed | tf_op | source)
XLA Modules:
  0.0 47.0 jit_solution(12328695589326634566)
XLA Ops:
  0.0 45.5 %shard_map.64 = bf16[4,8,8,256]{3,2,1,0:T(8,128)(2,1)} custom-call(bf16[8,16,16,128]{3,2,1,0:T(8,128)(2,1)} %v.1, bf16[9,384,128]{2,1,0:T(8,128)(2,1)} %bitcast.9, bf16[27,128,256]{2,1,0:T(8,128)(2,1)} %bitcast.7, bf16[27,256,128]{2,1,0:T(8,128)(2,1)} %bitcast.8, bf16[27,512,128]{2,1,0:T(8,128)(2,1)} %bitcast.6, bf16[27,768,256]{2,1,0:T(8,128)(2,1)} %bitcast.5), custom_call_target="tpu_custom_call" | custom-call | tf_op jit(solution)/shard_map/pallas_call | solution.py:469
  45.5 1.6 %copy.8 = bf16[4,8,8,256]{3,2,1,0:T(8,128)(2,1)} copy(bf16[4,8,8,256]{3,2,1,0:T(8,128)(2,1)} %shard_map.64) | data formatting | bytes 262144

commit v2 on v1

--- a/solution.py
+++ b/solution.py
@@ -22,9 +22,9 @@
 
 def kernel(
     dims,
-    v, wf_h, wh_h, w1_h, w2_h, wu_h,
+    v_h, wf_h, wh_h, w1_h, w2_h, wu_h,
     out,
-    wf, wh, w1, w2, wu, wsem, wt,
+    wf, wh, w1, w2, wu, wsem, vsem, wt,
     p1, f1, g1, e1, t1,
     p2, f2, g2, e2,
     p3, f3, g3, e3, acc,
@@ -35,6 +35,9 @@
     gx, gy, gz = lax.axis_index("gx"), lax.axis_index("gy"), lax.axis_index("gz")
     oz = 1 - gz
 
+    nx, ny, nz, c0 = v_h.shape
+    fetch = pltpu.make_async_copy(v_h, p1.at[1 : nx + 1, 1 : ny + 1], vsem)
+    fetch.start()
     loads = [
         pltpu.make_async_copy(src, dst, wsem.at[i])
         for i, (src, dst) in enumerate(((wf_h, wf), (wh_h, wh), (w1_h, w1), (w2_h, w2), (wu_h, wu)))
@@ -62,9 +65,14 @@
             return True
         return functools.reduce(jnp.logical_and, conds)
 
-    for ref in (p1, g1, p2, g2, p3, g3, l2, l3, l4):
+    for x in (0, nx + 1):
+        p1[x] = jnp.zeros(p1.shape[1:], BF16)
+    for y in (0, ny + 1):
+        p1[1 : nx + 1, y] = jnp.zeros((nx, nz, c0), BF16)
+    for ref in (g1, p2, g2, p3, g3, l2, l3, l4):
         ref[...] = jnp.zeros(ref.shape, ref.dtype)
 
+    fetch.wait()
     barrier = pltpu.get_barrier_semaphore()
     for s in range(gxn):
         there = lax.rem(gx + s, gxn)
@@ -153,11 +161,9 @@
     def rounded(x):
         return x.astype(BF16).astype(F32)
 
-    nx, ny, nz, c0 = v.shape
     for x in range(nx):
-        f1[x] = edge(v[x].astype(F32))
-    arrived = neighbours(v, 0, f1, p1, g1, nx, ny, s1, r1)
-    p1[1 : nx + 1, 1 : ny + 1] = v[...]
+        f1[x] = edge(p1[x + 1, 1 : ny + 1].astype(F32))
+    arrived = neighbours(p1, 1, f1, p1, g1, nx, ny, s1, r1)
 
     loads[0].wait()
     k0 = 3 * c0
@@ -451,7 +457,7 @@
     ]
     vm = pltpu.VMEM
     dma = pltpu.SemaphoreType.DMA
-    scratch = [vm(w.shape, BF16) for w in weights] + [dma((5,)), vm((3, 12 * c0, 2 * c0), BF16)]
+    scratch = [vm(w.shape, BF16) for w in weights] + [dma((5,)), dma(()), vm((3, 12 * c0, 2 * c0), BF16)]
     scratch += [
         vm((nx + 2, ny + 2, nz, c0), BF16), vm((nx, ny, 1, c0), F32), vm((nx + 2, ny + 2, 1, c0), F32),
         vm((nx + 2, ny + 2, nz, 3 * c0), BF16), vm((hy, nz, c0), F32),
@@ -469,13 +475,13 @@
     return pl.pallas_call(
         functools.partial(kernel, dims),
         out_shape=jax.ShapeDtypeStruct((hx, hy, hz, c1), BF16),
-        in_specs=[pl.BlockSpec(memory_space=pltpu.VMEM)] + [pl.BlockSpec(memory_space=pl.ANY)] * 5,
+        in_specs=[pl.BlockSpec(memory_space=pltpu.HBM)] * 6,
         out_specs=pl.BlockSpec(memory_space=pltpu.VMEM),
         scratch_shapes=scratch,
         compiler_params=pltpu.CompilerParams(
-            collective_id=0, has_side_effects=True, vmem_limit_bytes=60 * 1024 * 1024
+            collective_id=0, has_side_effects=True, vmem_limit_bytes=52 * 1024 * 1024
         ),
-    )(volume, *weights)
+    )(*[pltpu.with_memory_space_constraint(a, pltpu.HBM) for a in (volume, *weights)])
 
 
 def solution(mesh):

time: 47.3 us -> 47.7 us (level)
  Pallas kernels: 45.5 us -> 46.8 us
  local copies, waits for them, and re-layouts: 1.57 us -> 0.66 us
    pallas_call x1, Pallas kernels: 45.5 us -> 46.8 us  [on_device(): pl.pallas_call(functools.partial(kernel, dims), out_shape=jax.ShapeDtypeS...]
    unnamed x1, local copies, waits for them, and re-layouts: 1.57 us -> 0.66 us
where the time goes in v2:
time: 47.7 us; the launch traced here: 47.5 us
  Pallas kernels  46.8 us (98%)
  local copies, waits for them, and re-layouts  0.66 us (1%)
    pallas_call x1, Pallas kernels, on_device(): pl.pallas_call(functools.partial(kernel, dims), out_shape=jax.ShapeDtypeS...  46.8 us

profile of v2, /device:TPU:0, one launch (start us, length us, event | category | flops | bytes accessed | tf_op | source)
XLA Modules:
  0.0 47.5 jit_solution(4521896721110437952)
XLA Ops:
  0.0 46.8 %shard_map.64 = bf16[4,8,8,256]{3,2,1,0:T(8,128)(2,1)S(1)} custom-call(bf16[8,16,16,128]{3,2,1,0:T(8,128)(2,1)} %v_h.1, bf16[9,384,128]{2,1,0:T(8,128)(2,1)} %bitcast.9, bf16[27,128,256]{2,1,0:T(8,128)(2,1)} %bitcast.7, bf16[27,256,128]{2,1,0:T(8,128)(2,1)} %bitcast.8, bf16[27,512,128]{2,1,0:T(8,128)(2,1)} %bitcast.6, bf16[27,768,256]{2,1,0:T(8,128)(2,1)} %bitcast.5), custom_call_target="tpu_custom_call" | custom-call | tf_op jit(solution)/shard_map/pallas_call | solution.py:475
  46.8 0.7 %copy.8 = bf16[4,8,8,256]{3,2,1,0:T(8,128)(2,1)} copy(bf16[4,8,8,256]{3,2,1,0:T(8,128)(2,1)S(1)} %shard_map.64) | data formatting | bytes 262144

commit v3 on v2

--- a/solution.py
+++ b/solution.py
@@ -24,11 +24,11 @@
     dims,
     v_h, wf_h, wh_h, w1_h, w2_h, wu_h,
     out,
-    wf, wh, w1, w2, wu, wsem, vsem, wt,
-    p1, f1, g1, e1, t1,
-    p2, f2, g2, e2,
-    p3, f3, g3, e3, acc,
-    pk2, l2, sel2, q2, pk3, l3, q3, pk4, l4, vup,
+    wf, wh, w1, w2, wus, wuu, wsem, vsem, wt, wz,
+    p1, f1, g1, gs, e1, a1, rz, t1,
+    p2, f2, g2, e2, o2,
+    p3, f3, g3, e3, o3, acc,
+    pk2, l2, sel2, q2, b2, pk3, l3, q3, b3, pk4, l4, up, uo,
     s1, r1, s2, r2, s3, r3, s4, r4, s5, r5, s6, r6,
 ):
     gxn, gyn = dims
@@ -38,12 +38,13 @@
     nx, ny, nz, c0 = v_h.shape
     fetch = pltpu.make_async_copy(v_h, p1.at[1 : nx + 1, 1 : ny + 1], vsem)
     fetch.start()
+    c2 = w2.shape[1]
     loads = [
         pltpu.make_async_copy(src, dst, wsem.at[i])
-        for i, (src, dst) in enumerate(((wf_h, wf), (wh_h, wh), (w1_h, w1), (w2_h, w2), (wu_h, wu)))
+        for i, (src, dst) in enumerate((
+            (wf_h, wf), (wh_h, wh), (w1_h, w1), (w2_h, w2), (wu_h.at[:, c2:], wus), (wu_h.at[:, :c2], wuu),
+        ))
     ]
-    for load in loads:
-        load.start()
 
     def on(cond, fn):
         if cond is True:
@@ -72,7 +73,6 @@
     for ref in (g1, p2, g2, p3, g3, l2, l3, l4):
         ref[...] = jnp.zeros(ref.shape, ref.dtype)
 
-    fetch.wait()
     barrier = pltpu.get_barrier_semaphore()
     for s in range(gxn):
         there = lax.rem(gx + s, gxn)
@@ -90,6 +90,17 @@
 
                 on(exists(0, dy), signal)
     lines = 1 + (gy > 0).astype(jnp.int32) + (gy < gyn - 1).astype(jnp.int32)
+
+    def edge(block):
+        size = block.shape[-2]
+        rows = lax.broadcasted_iota(jnp.int32, block.shape, block.ndim - 2)
+        return jnp.sum(jnp.where(rows == (size - 1) * oz, block, 0.0), axis=block.ndim - 2, keepdims=True)
+
+    fetch.wait()
+    for load in loads:
+        load.start()
+    for x in range(nx):
+        f1[x] = edge(p1[x + 1, 1 : ny + 1].astype(F32))
     pl.semaphore_wait(barrier, 2 * gxn * lines - 1)
 
     def send(src, dst, ss, rs, x, y, z):
@@ -141,11 +152,6 @@
         late.append(lambda: finish(ss))
         return lambda: finish(rs)
 
-    def edge(block):
-        size = block.shape[-2]
-        rows = lax.broadcasted_iota(jnp.int32, block.shape, block.ndim - 2)
-        return jnp.sum(jnp.where(rows == (size - 1) * oz, block, 0.0), axis=block.ndim - 2, keepdims=True)
-
     def shifted(block, fill):
         size = block.shape[-2]
         axis = block.ndim - 2
@@ -161,41 +167,78 @@
     def rounded(x):
         return x.astype(BF16).astype(F32)
 
-    for x in range(nx):
-        f1[x] = edge(p1[x + 1, 1 : ny + 1].astype(F32))
     arrived = neighbours(p1, 1, f1, p1, g1, nx, ny, s1, r1)
 
+    k0 = 3 * c0
+    for x in (0, nx + 1):
+        e1[x] = jnp.zeros(e1.shape[1:], BF16)
+    for y in (0, ny + 1):
+        e1[1 : nx + 1, y] = jnp.zeros((nx, nz, k0), BF16)
+
+    def widen(at, block):
+        block = block.astype(F32)
+        below, above = shifted(block, None)
+        for k, part in enumerate((below, block, above)):
+            e1[at + (slice(None), pl.ds(k * c0, c0))] = part.astype(BF16)
+
+    @pl.loop(1, nx + 1)
+    def _(x):
+        widen((x, pl.ds(1, ny)), p1[x, 1 : ny + 1])
+
     loads[0].wait()
-    k0 = 3 * c0
     for oy in range(3):
         for plane in range(4):
             at = pl.ds(plane * k0, k0)
             wt[oy, at, :c0] = wf[plane * 3 + oy] if plane < 3 else jnp.zeros((k0, c0), BF16)
             wt[oy, at, c0:] = wf[(plane - 1) * 3 + oy] if plane > 0 else jnp.zeros((k0, c0), BF16)
-    arrived()
-
-    @pl.loop(0, nx + 2)
+    for tap in range(9):
+        wz[pl.ds(tap * c0, c0)] = wf[tap, pl.ds(pl.multiple_of(2 * oz * c0, c0), c0)]
+
+    @pl.loop(0, nx // 2)
     def _(x):
-        block = p1[x].astype(F32)
-        below, above = shifted(block, g1[x])
-        e1[x, :, :, 0:c0] = below.astype(BF16)
-        e1[x, :, :, c0 : 2 * c0] = p1[x]
-        e1[x, :, :, 2 * c0 :] = above.astype(BF16)
-
-    def full_rows(x):
         total = jnp.zeros((ny * nz, 2 * c0), F32)
         for oy in range(3):
             for half in range(2):
-                lhs = [e1[x + 2 * half + i, oy : oy + ny].reshape(ny * nz, k0) for i in range(2)]
+                lhs = [e1[2 * x + 2 * half + i, oy : oy + ny].reshape(ny * nz, k0) for i in range(2)]
                 rhs = wt[oy, 2 * half * k0 : 2 * (half + 1) * k0]
                 total = total + jnp.dot(jnp.concatenate(lhs, axis=1), rhs, preferred_element_type=F32)
-        return jnp.maximum(jnp.maximum(total[:, :c0], total[:, c0:]), 0.0)
+        a1[x] = total
+
+    arrived()
+    for x in range(nx + 2):
+        for y in range(ny + 2):
+            gs[x, y : y + 1] = g1[x, y]
+    lhs = [gs[ox : ox + nx, oy : oy + ny].reshape(nx * ny, c0).astype(BF16) for ox in range(3) for oy in range(3)]
+    rz[...] = jnp.dot(jnp.concatenate(lhs, axis=1), wz[...], preferred_element_type=F32)
+    for x, ox, lane in ((0, 0, 0), (nx + 1, 2, c0)):
+        widen((x, pl.ds(1, ny)), p1[x, 1 : ny + 1])
+        lhs = [e1[x, oy : oy + ny].reshape(ny * nz, k0) for oy in range(3)]
+        rhs = wf[ox * 3 : ox * 3 + 3].reshape(3 * k0, c0)
+        part = jnp.dot(jnp.concatenate(lhs, axis=1), rhs, preferred_element_type=F32)
+        at = (0 if ox == 0 else nx // 2 - 1, slice(None), pl.ds(lane, c0))
+        a1[at] = a1[at] + part
+    for y, oy in ((0, 0), (ny + 1, 2)):
+        widen((pl.ds(0, nx + 2), y), p1[:, y])
+        lhs = [e1[ox : ox + nx, y].reshape(nx * nz, k0) for ox in range(3)]
+        rhs = jnp.concatenate([wf[ox * 3 + oy] for ox in range(3)], axis=0)
+        part = jnp.dot(jnp.concatenate(lhs, axis=1), rhs, preferred_element_type=F32).reshape(nx, nz, c0)
+        for x in range(nx):
+            at = (x // 2, pl.ds((0 if oy == 0 else ny - 1) * nz, nz), pl.ds(x % 2 * c0, c0))
+            a1[at] = a1[at] + part[x]
+    tile = 8
+    last = lax.broadcasted_iota(jnp.int32, (tile, c0), 0) == (tile - 1) * oz
+    for x in range(nx):
+        for y in range(ny):
+            at = (x // 2, pl.ds(pl.multiple_of(y * nz + (nz - tile) * oz, tile), tile), pl.ds(x % 2 * c0, c0))
+            row = jnp.broadcast_to(rz[x * ny + y : x * ny + y + 1], (tile, c0))
+            a1[at] = a1[at] + jnp.where(last, row, 0.0)
 
     hx, hy, hz = nx // 2, ny // 2, nz // 2
 
     @pl.loop(0, hx)
     def _(x):
-        both = full_rows(2 * x).reshape(hy, 2, nz, c0)
+        total = a1[x]
+        both = jnp.maximum(jnp.maximum(total[:, :c0], total[:, c0:]), 0.0).reshape(hy, 2, nz, c0)
         t1[...] = jnp.max(both, axis=1)
         small = jnp.maximum(t1[:, pl.ds(0, hz, stride=2), :], t1[:, pl.ds(1, hz, stride=2), :])
         small = rounded(small)
@@ -204,19 +247,31 @@
 
     arrived = neighbours(p2, 1, f2, p2, g2, hx, hy, s2, r2)
     arrived()
-    for x in range(hx + 2):
-        block = p2[x]
-        below, above = shifted(block, g2[x])
-        e2[0, x], e2[1, x], e2[2, x] = below, block, above
+    rows = hx * hy * hz
+
+    def pack(even, odd, at, block, lane):
+        n, size, c = block.shape
+        even[at, :, :, pl.ds(lane, c)] = block.reshape(n * size, c).astype(BF16).reshape(n // 2, 2 * size, c)
+        block = block[1 : n - 1]
+        odd[at, :, :, pl.ds(lane, c)] = block.reshape((n - 2) * size, c).astype(BF16).reshape(n // 2 - 1, 2 * size, c)
+
+    def conv(even, odd, p, g, w):
+        for x in range(hx + 2):
+            block = p[x]
+            c = block.shape[-1]
+            below, above = shifted(block, g[x])
+            for k, part in enumerate((below, block, above)):
+                pack(even, odd, x, part, k * c)
+        total = jnp.zeros((rows, w.shape[2]), F32)
+        for ox in range(3):
+            lhs = [r[ox : ox + hx, lo : lo + hy // 2].reshape(rows, 3 * c) for r, lo in ((even, 0), (odd, 0), (even, 1))]
+            rhs = w[ox * 9 : ox * 9 + 9].reshape(9 * c, w.shape[2])
+            total = total + jnp.dot(jnp.concatenate(lhs, axis=1), rhs, preferred_element_type=F32)
+        return total
+
     loads[1].wait()
-    rows = hx * hy * hz
     c1 = wh.shape[2]
-    total = jnp.zeros((rows, c1), F32)
-    for ox in range(3):
-        for oy in range(3):
-            for k in range(3):
-                lhs = e2[k, ox : ox + hx, oy : oy + hy].reshape(rows, c0).astype(BF16)
-                total = total + jnp.dot(lhs, wh[(ox * 3 + oy) * 3 + k], preferred_element_type=F32)
+    total = conv(e2, o2, p2, g2, wh)
     skip = rounded(jnp.maximum(total, 0.0)).reshape(hx, hy, hz, c1)
     p3[1 : hx + 1, 1 : hy + 1] = skip
     f3[...] = edge(skip)
@@ -347,42 +402,41 @@
     landed = l2[...].astype(F32).reshape(width, c1).astype(BF16)
     block = jnp.dot(select, landed, preferred_element_type=F32).reshape(cy + 2, cz + 2, ax, c1)
 
-    def spread(q, block):
-        below, above = shifted(block, None)
-        q[0], q[1], q[2] = below, block, above
-
     deep = cy * cz * ax
     fo = w1.shape[2]
 
-    def bottom(q, w):
+    def spread(even, odd, block):
+        below, above = shifted(block, None)
+        c = block.shape[-1]
+        for ox, part in enumerate((below, block, above)):
+            whole = part.reshape((cy + 2) * (cz + 2) * ax, c).astype(BF16)
+            even[ox] = whole.reshape(cy + 2, cz // 2 + 1, 2 * ax, c)
+            inner = part[:, 1 : cz + 1].reshape((cy + 2) * cz * ax, c).astype(BF16)
+            odd[ox] = inner.reshape(cy + 2, cz // 2, 2 * ax, c)
+
+    def bottom(even, odd, w):
         total = jnp.zeros((deep, fo), F32)
+        c = even.shape[-1]
         for ox in range(3):
-            for oy in range(3):
-                for k in range(3):
-                    lhs = q[ox, oy : oy + cy, k : k + cz].reshape(deep, q.shape[-1]).astype(BF16)
-                    total = total + jnp.dot(lhs, w[(ox * 3 + oy) * 3 + k], preferred_element_type=F32)
+            lhs = [
+                r[ox, oy : oy + cy, lo : lo + cz // 2].reshape(deep, c)
+                for oy in range(3)
+                for r, lo in ((even, 0), (odd, 0), (even, 1))
+            ]
+            rhs = w[ox * 9 : ox * 9 + 9].reshape(9 * c, fo)
+            total = total + jnp.dot(jnp.concatenate(lhs, axis=1), rhs, preferred_element_type=F32)
         return jnp.maximum(total, 0.0).reshape(cy, cz, ax, fo).astype(BF16)
 
-    spread(q2, block)
+    spread(q2, b2, block)
     loads[2].wait()
-    first = bottom(q2, w1)
+    first = bottom(q2, b2, w1)
     pk3[...] = first
     l3[gx, 1 : cy + 1, 1 : cz + 1] = first
     arrived = column_exchange(deep_copy(pk3, l3, s5, r5), *blocks_of(l3, (s5, r5)))
 
     skip_arrived()
-    for x in range(hx + 2):
-        block = p3[x]
-        below, above = shifted(block, g3[x])
-        e3[0, x], e3[1, x], e3[2, x] = below, block, above
     loads[4].wait()
-    c2 = w2.shape[1]
-    total = jnp.zeros((rows, c1), F32)
-    for ox in range(3):
-        for oy in range(3):
-            for k in range(3):
-                lhs = e3[k, ox : ox + hx, oy : oy + hy].reshape(rows, c1).astype(BF16)
-                total = total + jnp.dot(lhs, wu[(ox * 3 + oy) * 3 + k, c2:, :], preferred_element_type=F32)
+    total = conv(e3, o3, p3, g3, wus)
     acc[...] = total.reshape(hx, hy, hz, c1)
 
     near = cx + 2
@@ -401,12 +455,14 @@
     for k in range(3):
         for x in range(-1, hx + 1):
             blocks.append(jnp.where(lane == (((zs + (k - 1)) >> 1) + 2) * near + (x >> 1) + 1, 1.0, 0.0))
+    for k in range(3):
+        blocks += blocks[k * (hx + 2) + 1 : (k + 1) * (hx + 2) - 1]
     pick = jnp.concatenate(blocks, axis=0).astype(BF16)
 
     arrived()
-    spread(q3, jnp.concatenate([l3[g].astype(F32) for g in range(gxn)], axis=-1))
+    spread(q3, b3, jnp.concatenate([l3[g].astype(F32) for g in range(gxn)], axis=-1))
     loads[3].wait()
-    second = bottom(q3, w2)
+    second = bottom(q3, b3, w2)
     for y in range(cy):
         line = second[y].astype(F32).reshape(cz * ax, fo).astype(BF16)
         line = jnp.dot(share, line, preferred_element_type=F32)
@@ -414,20 +470,28 @@
     l4[gx, 1 : cy + 1, 1 : cz // 2 + 1] = pk4[gx]
     arrived = column_exchange(narrow_copy, *blocks_of(l4, (s6, r6)))
     arrived()
+    rows_o = hx * hz
+    loads[5].wait()
     for y in range(cy + 2):
         field = jnp.concatenate([l4[g, y].astype(F32) for g in range(gxn)], axis=-1)
         field = field.reshape((cz + 4) * near, c2).astype(BF16)
-        vup[:, y] = jnp.dot(pick, field, preferred_element_type=F32).reshape(3, hx + 2, hz, c2)
+        field = jnp.dot(pick, field, preferred_element_type=F32).astype(BF16)
+        for k in range(3):
+            size = (hx + 2) * hz
+            part = field[k * size : (k + 1) * size]
+            up[y, :, :, pl.ds(k * c2, c2)] = part.reshape(hx // 2 + 1, 2 * hz, c2)
+            part = field[3 * size + k * rows_o : 3 * size + (k + 1) * rows_o]
+            uo[y, :, :, pl.ds(k * c2, c2)] = part.reshape(hx // 2, 2 * hz, c2)
 
     parts = []
     for oy in range(3):
         low, high = (oy + 1) // 2, (hy - 1 + oy + 1) // 2 + 1
         count = high - low
         total = jnp.zeros((count * hx * hz, c1), F32)
-        for ox in range(3):
-            for k in range(3):
-                lhs = vup[k, low:high, ox : ox + hx].reshape(count * hx * hz, c2).astype(BF16)
-                total = total + jnp.dot(lhs, wu[(ox * 3 + oy) * 3 + k, :c2, :], preferred_element_type=F32)
+        for ox, (r, lo) in enumerate(((up, 0), (uo, 0), (up, 1))):
+            lhs = r[low:high, lo : lo + hx // 2].reshape(count * hx * hz, 3 * c2)
+            rhs = wuu[(ox * 3 + oy) * 3 : (ox * 3 + oy) * 3 + 3].reshape(3 * c2, c1)
+            total = total + jnp.dot(lhs, rhs, preferred_element_type=F32)
         parts.append((low, total.reshape(count, hx, hz, c1)))
     for y in range(hy):
         line = acc[:, y]
@@ -457,19 +521,25 @@
     ]
     vm = pltpu.VMEM
     dma = pltpu.SemaphoreType.DMA
-    scratch = [vm(w.shape, BF16) for w in weights] + [dma((5,)), dma(()), vm((3, 12 * c0, 2 * c0), BF16)]
+    scratch = [vm(w.shape, BF16) for w in weights[:4]]
+    scratch += [vm((27, c1, c1), BF16), vm((27, c2, c1), BF16), dma((6,)), dma(())]
+    scratch += [vm((3, 12 * c0, 2 * c0), BF16), vm((9 * c0, c0), BF16)]
     scratch += [
         vm((nx + 2, ny + 2, nz, c0), BF16), vm((nx, ny, 1, c0), F32), vm((nx + 2, ny + 2, 1, c0), F32),
-        vm((nx + 2, ny + 2, nz, 3 * c0), BF16), vm((hy, nz, c0), F32),
+        vm((nx + 2, ny + 2, c0), F32), vm((nx + 2, ny + 2, nz, 3 * c0), BF16), vm((hx, ny * nz, 2 * c0), F32),
+        vm((nx * ny, c0), F32), vm((hy, nz, c0), F32),
         vm((hx + 2, hy + 2, hz, c0), F32), vm((hx, hy, 1, c0), F32), vm((hx + 2, hy + 2, 1, c0), F32),
-        vm((3, hx + 2, hy + 2, hz, c0), F32),
+        vm((hx + 2, hy // 2 + 1, 2 * hz, 3 * c0), BF16), vm((hx + 2, hy // 2, 2 * hz, 3 * c0), BF16),
         vm((hx + 2, hy + 2, hz, c1), F32), vm((hx, hy, 1, c1), F32), vm((hx + 2, hy + 2, 1, c1), F32),
-        vm((3, hx + 2, hy + 2, hz, c1), F32), vm((hx, hy, hz, c1), F32),
+        vm((hx + 2, hy // 2 + 1, 2 * hz, 3 * c1), BF16), vm((hx + 2, hy // 2, 2 * hz, 3 * c1), BF16),
+        vm((hx, hy, hz, c1), F32),
         vm((cy + 1, cz * cx, c1), BF16), vm((gxn, cy + 5, cz * cx, c1), BF16),
-        vm((cy + 2, cz + 2, ax, gxn * (cy + 5) * cz * cx), F32), vm((3, cy + 2, cz + 2, ax, c1), F32),
-        vm((cy, cz, ax, fo), BF16), vm((gxn, cy + 2, cz + 2, ax, fo), BF16), vm((3, cy + 2, cz + 2, ax, c2), F32),
+        vm((cy + 2, cz + 2, ax, gxn * (cy + 5) * cz * cx), F32),
+        vm((3, cy + 2, cz // 2 + 1, 2 * ax, c1), BF16), vm((3, cy + 2, cz // 2, 2 * ax, c1), BF16),
+        vm((cy, cz, ax, fo), BF16), vm((gxn, cy + 2, cz + 2, ax, fo), BF16),
+        vm((3, cy + 2, cz // 2 + 1, 2 * ax, c2), BF16), vm((3, cy + 2, cz // 2, 2 * ax, c2), BF16),
         vm((gxn, cy, cz // 2, 2 * (cx + 2), fo), BF16), vm((gxn, cy + 2, cz // 2 + 2, 2 * (cx + 2), fo), BF16),
-        vm((3, cy + 2, hx + 2, hz, c2), F32),
+        vm((cy + 2, hx // 2 + 1, 2 * hz, 3 * c2), BF16), vm((cy + 2, hx // 2, 2 * hz, 3 * c2), BF16),
     ]
     scratch += [dma((3,))] * 12
     return pl.pallas_call(

time: 47.7 us -> 41.7 us (0.87)
  Pallas kernels: 46.8 us -> 40.9 us
    pallas_call x1, Pallas kernels: 46.8 us -> 40.9 us  [on_device(): pl.pallas_call(functools.partial(kernel, dims), out_shape=jax.ShapeDtypeS...]
where the time goes in v3:
time: 41.7 us; the launch traced here: 41.6 us
  Pallas kernels  40.9 us (98%)
  local copies, waits for them, and re-layouts  0.66 us (2%)
    pallas_call x1, Pallas kernels, on_device(): pl.pallas_call(functools.partial(kernel, dims), out_shape=jax.ShapeDtypeS...  40.9 us

profile of v3, /device:TPU:0, one launch (start us, length us, event | category | flops | bytes accessed | tf_op | source)
XLA Modules:
  0.0 41.6 jit_solution(18091521936297195717)
XLA Ops:
  0.0 40.9 %shard_map.64 = bf16[4,8,8,256]{3,2,1,0:T(8,128)(2,1)S(1)} custom-call(bf16[8,16,16,128]{3,2,1,0:T(8,128)(2,1)} %v_h.1, bf16[9,384,128]{2,1,0:T(8,128)(2,1)} %bitcast.9, bf16[27,128,256]{2,1,0:T(8,128)(2,1)} %bitcast.7, bf16[27,256,128]{2,1,0:T(8,128)(2,1)} %bitcast.8, bf16[27,512,128]{2,1,0:T(8,128)(2,1)} %bitcast.6, bf16[27,768,256]{2,1,0:T(8,128)(2,1)} %bitcast.5), custom_call_target="tpu_custom_call" | custom-call | tf_op jit(solution)/shard_map/pallas_call | solution.py:545
  40.9 0.7 %copy.8 = bf16[4,8,8,256]{3,2,1,0:T(8,128)(2,1)} copy(bf16[4,8,8,256]{3,2,1,0:T(8,128)(2,1)S(1)} %shard_map.64) | data formatting | bytes 262144

commit v4 on v3

--- a/solution.py
+++ b/solution.py
@@ -28,7 +28,7 @@
     p1, f1, g1, gs, e1, a1, rz, t1,
     p2, f2, g2, e2, o2,
     p3, f3, g3, e3, o3, acc,
-    pk2, l2, sel2, q2, b2, pk3, l3, q3, b3, pk4, l4, up, uo,
+    pk2, l2, m2, sel2, selm, q2, b2, pk3, l3, q3, b3, pk4, l4, up, sums, deeps, thirds,
     s1, r1, s2, r2, s3, r3, s4, r4, s5, r5, s6, r6,
 ):
     gxn, gyn = dims
@@ -70,7 +70,7 @@
         p1[x] = jnp.zeros(p1.shape[1:], BF16)
     for y in (0, ny + 1):
         p1[1 : nx + 1, y] = jnp.zeros((nx, nz, c0), BF16)
-    for ref in (g1, p2, g2, p3, g3, l2, l3, l4):
+    for ref in (g1, m2, l3, l4):
         ref[...] = jnp.zeros(ref.shape, ref.dtype)
 
     barrier = pltpu.get_barrier_semaphore()
@@ -96,6 +96,13 @@
         rows = lax.broadcasted_iota(jnp.int32, block.shape, block.ndim - 2)
         return jnp.sum(jnp.where(rows == (size - 1) * oz, block, 0.0), axis=block.ndim - 2, keepdims=True)
 
+    for ref in (g2, g3):
+        ref[...] = jnp.zeros(ref.shape, ref.dtype)
+    for ref in (p2, p3):
+        for x in (0, ref.shape[0] - 1):
+            ref[x] = jnp.zeros(ref.shape[1:], BF16)
+        for y in (0, ref.shape[1] - 1):
+            ref[:, y] = jnp.zeros(ref.shape[:1] + ref.shape[2:], BF16)
     fetch.wait()
     for load in loads:
         load.start()
@@ -242,7 +249,7 @@
         t1[...] = jnp.max(both, axis=1)
         small = jnp.maximum(t1[:, pl.ds(0, hz, stride=2), :], t1[:, pl.ds(1, hz, stride=2), :])
         small = rounded(small)
-        p2[x + 1, 1 : hy + 1] = small
+        p2[x + 1, 1 : hy + 1] = small.astype(BF16)
         f2[x] = edge(small)
 
     arrived = neighbours(p2, 1, f2, p2, g2, hx, hy, s2, r2)
@@ -257,23 +264,29 @@
 
     def conv(even, odd, p, g, w):
         for x in range(hx + 2):
-            block = p[x]
+            block = p[x].astype(F32)
             c = block.shape[-1]
             below, above = shifted(block, g[x])
             for k, part in enumerate((below, block, above)):
                 pack(even, odd, x, part, k * c)
-        total = jnp.zeros((rows, w.shape[2]), F32)
-        for ox in range(3):
-            lhs = [r[ox : ox + hx, lo : lo + hy // 2].reshape(rows, 3 * c) for r, lo in ((even, 0), (odd, 0), (even, 1))]
-            rhs = w[ox * 9 : ox * 9 + 9].reshape(9 * c, w.shape[2])
-            total = total + jnp.dot(jnp.concatenate(lhs, axis=1), rhs, preferred_element_type=F32)
-        return total
+        sums[...] = jnp.zeros_like(sums)
+
+        @pl.loop(0, 3)
+        def _(ox):
+            total = sums[...]
+            for oy, (r, lo) in enumerate(((even, 0), (odd, 0), (even, 1))):
+                lhs = r[pl.ds(ox, hx), lo : lo + hy // 2].reshape(rows, 3 * c)
+                rhs = w[pl.ds(ox * 9 + oy * 3, 3)].reshape(3 * c, w.shape[2])
+                total = total + jnp.dot(lhs, rhs, preferred_element_type=F32)
+            sums[...] = total
+
+        return sums[...]
 
     loads[1].wait()
     c1 = wh.shape[2]
     total = conv(e2, o2, p2, g2, wh)
     skip = rounded(jnp.maximum(total, 0.0)).reshape(hx, hy, hz, c1)
-    p3[1 : hx + 1, 1 : hy + 1] = skip
+    p3[1 : hx + 1, 1 : hy + 1] = skip.astype(BF16)
     f3[...] = edge(skip)
 
     cx, cy, cz = hx // 2, hy // 2, hz // 2
@@ -297,17 +310,17 @@
     pk2[...] = packets
     l2[gx, 0:cy] = packets[0:cy]
 
-    slots = cy + 5
-
     def coarse_copy(k, dy, z):
         def make(src_gx, tgt_gx):
             if z == 0:
                 src = {0: pl.ds(0, cy), -1: pl.ds(0, 1), 1: pl.ds(cy - 1, 1)}[dy]
-                dst = {0: pl.ds(0, cy), 1: pl.ds(cy, 1), -1: pl.ds(cy + 1, 1)}[dy]
             else:
                 src = pl.ds(cy, 1)
-                dst = {0: pl.ds(cy + 2, 1), 1: pl.ds(cy + 3, 1), -1: pl.ds(cy + 4, 1)}[dy]
-            return send(pk2.at[src], l2.at[src_gx, dst], s4.at[k], r4.at[k], tgt_gx, gy + dy, oz if z else gz)
+            if dy == 0:
+                dst = l2.at[src_gx, pl.ds(cy, 1) if z else pl.ds(0, cy)]
+            else:
+                dst = m2.at[src_gx, pl.ds(2 * z + (1 if dy < 0 else 0), 1)]
+            return send(pk2.at[src], dst, s4.at[k], r4.at[k], tgt_gx, gy + dy, oz if z else gz)
 
         return make
 
@@ -342,97 +355,132 @@
 
         return make
 
-    def column_exchange(choose, away, home):
-        for s in list(range(1, gxn)) + [0]:
-            there = lax.rem(gx + s, gxn)
-            for k, (dy, z) in enumerate(((0, 0), (-1, 0), (1, 0), (0, 1), (-1, 1), (1, 1))):
-                if s == 0 and k == 0:
-                    continue
-                on(exists(0, dy), choose(0 if s else 1 + z, dy, z)(gx, there).start)
-
-        def finish(which):
-            def both(b):
-                drain(*away(b, which))
-                for k in (0, 1):
-                    drain(*home(b, k, which))
-
-            by_y(both)
-
-        late.append(lambda: finish(0))
-        return lambda: finish(1)
-
-    def blocks_of(land, sems):
+    def column_exchange(choose, main, rim):
+        far = list(range(1, gxn))
+        for s, dy, z in (
+            [(s, 0, 0) for s in far]
+            + [(s, 0, 1) for s in far + [0]]
+            + [(s, dy, 0) for s in far + [0] for dy in (-1, 1)]
+            + [(s, dy, 1) for s in far + [0] for dy in (-1, 1)]
+        ):
+            k = 2 if dy else (0 if s else 1)
+            on(exists(0, dy), choose(k, dy, z)(gx, lax.rem(gx + s, gxn)).start)
+
+        def first(which):
+            for k, ref in enumerate(main):
+                drain(ref, which.at[k])
+
+        def second(which):
+            by_y(lambda b: drain(rim(b), which.at[2]))
+
+        return first, second
+
+    def leave(waits, sems):
+        late.append(lambda: [wait(sems) for wait in waits])
+        return waits
+
+    def parts_of(land):
         wz = land.shape[2] - 2
-
-        def away(b, which):
-            return land.at[0 : gxn - 1, 0 : cy + b, 0 : wz + 1], sems[which].at[0]
-
-        def home(b, k, which):
-            return land.at[0, 0 : (cy if k else 0) + b, 0 : 1 if k else wz], sems[which].at[1 + k]
-
-        return away, home
-
-    arrived = column_exchange(
-        coarse_copy,
-        lambda b, which: (l2.at[0 : gxn - 1, 0 : cy + 1 + 2 * b], (s4, r4)[which].at[0]),
-        lambda b, k, which: (l2.at[0, 0 : b + k], (s4, r4)[which].at[1 + k]),
+        main = (land.at[0 : gxn - 1, 0:cy, 0 : wz + 1], land.at[0, 0:cy, 0:1])
+        return main, lambda b: land.at[0:gxn, 0:b, 0 : wz + 1]
+
+    main4, rim4 = leave(
+        column_exchange(coarse_copy, (l2.at[0 : gxn - 1], l2.at[0, 0:1]), lambda b: m2.at[0:gxn, 0 : 2 * b]), s4
     )
 
-    span_g = slots * group
-    width = gxn * span_g
-    lane = lax.broadcasted_iota(jnp.int32, (ax, width), 1)
-    xs = lax.broadcasted_iota(jnp.int32, (ax, width), 0)
-    base = lane - ((xs >> shift_x) * span_g + (xs & (cx - 1)))
+    def one_hot(ref, at, slots):
+        width = gxn * slots * group
+        lane = lax.broadcasted_iota(jnp.int32, (ax, width), 1)
+        xs = lax.broadcasted_iota(jnp.int32, (ax, width), 0)
+        base = lane - ((xs >> shift_x) * slots * group + (xs & (cx - 1)))
+        ref[at] = jnp.where(base == slots_at, 1.0, 0.0)
+
     for y in range(-1, cy + 1):
         for z in range(-1, cz + 1):
+            inside = 0 <= y < cy
+            rim_slot = 0 if y < 0 else 1
             if 0 <= z < cz:
-                slot = y if 0 <= y < cy else (cy if y < 0 else cy + 1)
-                at = slot * group + z * cx
+                slots_at = (y if inside else rim_slot) * group + z * cx
             else:
-                slot = cy + 2 if 0 <= y < cy else (cy + 3 if y < 0 else cy + 4)
-                line = y if 0 <= y < cy else (cy - 1 if y < 0 else 0)
+                line = y if inside else (cy - 1 if y < 0 else 0)
                 mine = (gz == 1) if z < 0 else (gz == 0)
-                at = jnp.where(mine, slot * group + line * cx, -width * 4)
-            sel2[y + 1, z + 1] = jnp.where(base == at, 1.0, 0.0)
-
-    rim = (cy + 2) * (cz + 2) * ax
-    select = sel2[...].reshape(rim, width).astype(BF16)
-    arrived()
-    skip_arrived = neighbours(p3, 1, f3, p3, g3, hx, hy, s3, r3)
-    landed = l2[...].astype(F32).reshape(width, c1).astype(BF16)
-    block = jnp.dot(select, landed, preferred_element_type=F32).reshape(cy + 2, cz + 2, ax, c1)
+                slots_at = jnp.where(mine, (cy if inside else 2 + rim_slot) * group + line * cx, -(1 << 20))
+            if inside:
+                one_hot(sel2, (y, z + 1), cy + 1)
+            else:
+                one_hot(selm, (rim_slot, z + 1), 4)
+
+    def gathered(ref, land):
+        n, width = ref.shape[0], ref.shape[-1]
+        select = ref[...].reshape(n * (cz + 2) * ax, width).astype(BF16)
+        landed = land[...].astype(F32).reshape(width, c1).astype(BF16)
+        return jnp.dot(select, landed, preferred_element_type=F32).reshape(n, cz + 2, ax, c1)
 
     deep = cy * cz * ax
     fo = w1.shape[2]
 
-    def spread(even, odd, block):
+    windows = ((0, 0), (1, 0), (0, 1))
+
+    def spread(even, odd, block, row):
         below, above = shifted(block, None)
-        c = block.shape[-1]
+        n, c = block.shape[0], block.shape[-1]
         for ox, part in enumerate((below, block, above)):
-            whole = part.reshape((cy + 2) * (cz + 2) * ax, c).astype(BF16)
-            even[ox] = whole.reshape(cy + 2, cz // 2 + 1, 2 * ax, c)
-            inner = part[:, 1 : cz + 1].reshape((cy + 2) * cz * ax, c).astype(BF16)
-            odd[ox] = inner.reshape(cy + 2, cz // 2, 2 * ax, c)
-
-    def bottom(even, odd, w):
-        total = jnp.zeros((deep, fo), F32)
-        c = even.shape[-1]
-        for ox in range(3):
-            lhs = [
-                r[ox, oy : oy + cy, lo : lo + cz // 2].reshape(deep, c)
-                for oy in range(3)
-                for r, lo in ((even, 0), (odd, 0), (even, 1))
-            ]
-            rhs = w[ox * 9 : ox * 9 + 9].reshape(9 * c, fo)
-            total = total + jnp.dot(jnp.concatenate(lhs, axis=1), rhs, preferred_element_type=F32)
-        return jnp.maximum(total, 0.0).reshape(cy, cz, ax, fo).astype(BF16)
-
-    spread(q2, b2, block)
+            whole = part.reshape(n * (cz + 2) * ax, c).astype(BF16)
+            even[ox, row : row + n] = whole.reshape(n, cz // 2 + 1, 2 * ax, c)
+            inner = part[:, 1 : cz + 1].reshape(n * cz * ax, c).astype(BF16)
+            odd[ox, row : row + n] = inner.reshape(n, cz // 2, 2 * ax, c)
+
+    def window(pair, ox, row, n):
+        c = pair[0].shape[-1]
+        lhs = [pair[i][ox, row : row + n, lo : lo + cz // 2].reshape(n * cz * ax, c) for i, lo in windows]
+        return jnp.concatenate(lhs, axis=1)
+
+    def bottom_own(pair, w):
+        k = 3 * w.shape[1]
+        deeps[...] = jnp.zeros_like(deeps)
+
+        @pl.loop(0, 3)
+        def _(ox):
+            lhs = window(pair, ox, 1, cy)
+            rhs = [w[pl.ds(ox * 9 + oy * 3, 3)].reshape(k, fo) for oy in range(3)]
+            if fo % 128 == 0:
+                total = jnp.dot(lhs, jnp.concatenate(rhs, axis=1), preferred_element_type=F32)
+                total = [total[:, oy * fo : (oy + 1) * fo] for oy in range(3)]
+            else:
+                total = [jnp.dot(lhs, r, preferred_element_type=F32) for r in rhs]
+            for oy in range(3):
+                deeps[oy] = deeps[oy] + total[oy]
+
+    def bottom_rim(pair, w):
+        k = 3 * w.shape[1]
+        size = cz * ax
+        ends = []
+        for row, oy in ((0, 0), (cy + 1, 2)):
+            total = jnp.zeros((size, fo), F32)
+            for ox in range(3):
+                rhs = w[(ox * 3 + oy) * 3 : (ox * 3 + oy) * 3 + 3].reshape(k, fo)
+                total = total + jnp.dot(window(pair, ox, row, 1), rhs, preferred_element_type=F32)
+            ends.append(total)
+        lines = []
+        for y in range(cy):
+            before = deeps[0, (y - 1) * size : y * size] if y > 0 else ends[0]
+            after = deeps[2, (y + 1) * size : (y + 2) * size] if y < cy - 1 else ends[1]
+            lines.append(deeps[1, y * size : (y + 1) * size] + before + after)
+        return jnp.maximum(jnp.concatenate(lines, axis=0), 0.0).reshape(cy, cz, ax, fo).astype(BF16)
+
+    main4(r4)
+    skip_arrived = neighbours(p3, 1, f3, p3, g3, hx, hy, s3, r3)
+    spread(q2, b2, gathered(sel2, l2), 1)
     loads[2].wait()
-    first = bottom(q2, b2, w1)
+    bottom_own((q2, b2), w1)
+    rim4(r4)
+    block = gathered(selm, m2)
+    spread(q2, b2, block[0:1], 0)
+    spread(q2, b2, block[1:2], cy + 1)
+    first = bottom_rim((q2, b2), w1)
     pk3[...] = first
     l3[gx, 1 : cy + 1, 1 : cz + 1] = first
-    arrived = column_exchange(deep_copy(pk3, l3, s5, r5), *blocks_of(l3, (s5, r5)))
+    main5, rim5 = leave(column_exchange(deep_copy(pk3, l3, s5, r5), *parts_of(l3)), s5)
 
     skip_arrived()
     loads[4].wait()
@@ -459,46 +507,68 @@
         blocks += blocks[k * (hx + 2) + 1 : (k + 1) * (hx + 2) - 1]
     pick = jnp.concatenate(blocks, axis=0).astype(BF16)
 
-    arrived()
-    spread(q3, b3, jnp.concatenate([l3[g].astype(F32) for g in range(gxn)], axis=-1))
+    def joined(row, n):
+        return jnp.concatenate([l3[g, row : row + n].astype(F32) for g in range(gxn)], axis=-1)
+
+    main5(r5)
+    spread(q3, b3, joined(1, cy), 1)
     loads[3].wait()
-    second = bottom(q3, b3, w2)
+    bottom_own((q3, b3), w2)
+    rim5(r5)
+    spread(q3, b3, joined(0, 1), 0)
+    spread(q3, b3, joined(cy + 1, 1), cy + 1)
+    second = bottom_rim((q3, b3), w2)
     for y in range(cy):
         line = second[y].astype(F32).reshape(cz * ax, fo).astype(BF16)
         line = jnp.dot(share, line, preferred_element_type=F32)
         pk4[:, y] = line.reshape(gxn, cz // 2, 2 * near, fo).astype(BF16)
     l4[gx, 1 : cy + 1, 1 : cz // 2 + 1] = pk4[gx]
-    arrived = column_exchange(narrow_copy, *blocks_of(l4, (s6, r6)))
-    arrived()
-    rows_o = hx * hz
-    loads[5].wait()
-    for y in range(cy + 2):
+    main6, rim6 = leave(column_exchange(narrow_copy, *parts_of(l4)), s6)
+    size = hx * hz
+
+    def enlarge(y):
         field = jnp.concatenate([l4[g, y].astype(F32) for g in range(gxn)], axis=-1)
         field = field.reshape((cz + 4) * near, c2).astype(BF16)
         field = jnp.dot(pick, field, preferred_element_type=F32).astype(BF16)
         for k in range(3):
-            size = (hx + 2) * hz
-            part = field[k * size : (k + 1) * size]
-            up[y, :, :, pl.ds(k * c2, c2)] = part.reshape(hx // 2 + 1, 2 * hz, c2)
-            part = field[3 * size + k * rows_o : 3 * size + (k + 1) * rows_o]
-            uo[y, :, :, pl.ds(k * c2, c2)] = part.reshape(hx // 2, 2 * hz, c2)
-
-    parts = []
-    for oy in range(3):
-        low, high = (oy + 1) // 2, (hy - 1 + oy + 1) // 2 + 1
-        count = high - low
-        total = jnp.zeros((count * hx * hz, c1), F32)
-        for ox, (r, lo) in enumerate(((up, 0), (uo, 0), (up, 1))):
-            lhs = r[low:high, lo : lo + hx // 2].reshape(count * hx * hz, 3 * c2)
-            rhs = wuu[(ox * 3 + oy) * 3 : (ox * 3 + oy) * 3 + 3].reshape(3 * c2, c1)
-            total = total + jnp.dot(lhs, rhs, preferred_element_type=F32)
-        parts.append((low, total.reshape(count, hx, hz, c1)))
+            at = pl.ds(k * c2, c2)
+            part = field[k * (size + 2 * hz) : (k + 1) * (size + 2 * hz)]
+            up[0, y, :, :, at] = part[:size].reshape(hx // 2, 2 * hz, c2)
+            up[2, y, :, :, at] = part[2 * hz :].reshape(hx // 2, 2 * hz, c2)
+            part = field[3 * (size + 2 * hz) + k * size : 3 * (size + 2 * hz) + (k + 1) * size]
+            up[1, y, :, :, at] = part.reshape(hx // 2, 2 * hz, c2)
+
+    thirds[...] = jnp.zeros_like(thirds)
+    main6(r6)
+    for y in range(1, cy + 1):
+        enlarge(y)
+    loads[5].wait()
+
+    @pl.loop(0, 3)
+    def _(ox):
+        lhs = up[ox, 1 : cy + 1].reshape(cy * size, 3 * c2)
+        for oy in range(3):
+            rhs = wuu[pl.ds(ox * 9 + oy * 3, 3)].reshape(3 * c2, c1)
+            thirds[oy] = thirds[oy] + jnp.dot(lhs, rhs, preferred_element_type=F32)
+
     for y in range(hy):
         line = acc[:, y]
         for oy in range(3):
-            low, part = parts[oy]
-            line = line + part[(y + oy + 1) // 2 - low]
-        out[:, y] = line.astype(BF16)
+            at = (y + oy + 1) // 2 - 1
+            if 0 <= at < cy:
+                line = line + thirds[oy, at * size : (at + 1) * size].reshape(hx, hz, c1)
+        if 0 < y < hy - 1:
+            out[:, y] = line.astype(BF16)
+        else:
+            acc[:, y] = line
+    rim6(r6)
+    for row, oy, y in ((0, 0, 0), (cy + 1, 2, hy - 1)):
+        enlarge(row)
+        total = jnp.zeros((size, c1), F32)
+        for ox in range(3):
+            rhs = wuu[(ox * 3 + oy) * 3 : (ox * 3 + oy) * 3 + 3].reshape(3 * c2, c1)
+            total = total + jnp.dot(up[ox, row].reshape(size, 3 * c2), rhs, preferred_element_type=F32)
+        out[:, y] = (acc[:, y] + total.reshape(hx, hz, c1)).astype(BF16)
 
     for fn in late:
         fn()
@@ -528,18 +598,19 @@
         vm((nx + 2, ny + 2, nz, c0), BF16), vm((nx, ny, 1, c0), F32), vm((nx + 2, ny + 2, 1, c0), F32),
         vm((nx + 2, ny + 2, c0), F32), vm((nx + 2, ny + 2, nz, 3 * c0), BF16), vm((hx, ny * nz, 2 * c0), F32),
         vm((nx * ny, c0), F32), vm((hy, nz, c0), F32),
-        vm((hx + 2, hy + 2, hz, c0), F32), vm((hx, hy, 1, c0), F32), vm((hx + 2, hy + 2, 1, c0), F32),
+        vm((hx + 2, hy + 2, hz, c0), BF16), vm((hx, hy, 1, c0), F32), vm((hx + 2, hy + 2, 1, c0), F32),
         vm((hx + 2, hy // 2 + 1, 2 * hz, 3 * c0), BF16), vm((hx + 2, hy // 2, 2 * hz, 3 * c0), BF16),
-        vm((hx + 2, hy + 2, hz, c1), F32), vm((hx, hy, 1, c1), F32), vm((hx + 2, hy + 2, 1, c1), F32),
+        vm((hx + 2, hy + 2, hz, c1), BF16), vm((hx, hy, 1, c1), F32), vm((hx + 2, hy + 2, 1, c1), F32),
         vm((hx + 2, hy // 2 + 1, 2 * hz, 3 * c1), BF16), vm((hx + 2, hy // 2, 2 * hz, 3 * c1), BF16),
         vm((hx, hy, hz, c1), F32),
-        vm((cy + 1, cz * cx, c1), BF16), vm((gxn, cy + 5, cz * cx, c1), BF16),
-        vm((cy + 2, cz + 2, ax, gxn * (cy + 5) * cz * cx), F32),
+        vm((cy + 1, cz * cx, c1), BF16), vm((gxn, cy + 1, cz * cx, c1), BF16), vm((gxn, 4, cz * cx, c1), BF16),
+        vm((cy, cz + 2, ax, gxn * (cy + 1) * cz * cx), F32), vm((2, cz + 2, ax, gxn * 4 * cz * cx), F32),
         vm((3, cy + 2, cz // 2 + 1, 2 * ax, c1), BF16), vm((3, cy + 2, cz // 2, 2 * ax, c1), BF16),
         vm((cy, cz, ax, fo), BF16), vm((gxn, cy + 2, cz + 2, ax, fo), BF16),
         vm((3, cy + 2, cz // 2 + 1, 2 * ax, c2), BF16), vm((3, cy + 2, cz // 2, 2 * ax, c2), BF16),
         vm((gxn, cy, cz // 2, 2 * (cx + 2), fo), BF16), vm((gxn, cy + 2, cz // 2 + 2, 2 * (cx + 2), fo), BF16),
-        vm((cy + 2, hx // 2 + 1, 2 * hz, 3 * c2), BF16), vm((cy + 2, hx // 2, 2 * hz, 3 * c2), BF16),
+        vm((3, cy + 2, hx // 2, 2 * hz, 3 * c2), BF16),
+        vm((hx * hy * hz, c1), F32), vm((3, cy * cz * ax, fo), F32), vm((3, cy * hx * hz, c1), F32),
     ]
     scratch += [dma((3,))] * 12
     return pl.pallas_call(

time: 41.7 us -> 40.5 us (0.971)
  Pallas kernels: 40.9 us -> 39.7 us
    pallas_call x1, Pallas kernels: 40.9 us -> 39.7 us  [on_device(): pl.pallas_call(functools.partial(kernel, dims), out_shape=jax.ShapeDtypeS...]
where the time goes in v4:
time: 40.5 us; the launch traced here: 40.3 us
  Pallas kernels  39.7 us (98%)
  local copies, waits for them, and re-layouts  0.66 us (2%)
    pallas_call x1, Pallas kernels, on_device(): pl.pallas_call(functools.partial(kernel, dims), out_shape=jax.ShapeDtypeS...  39.7 us

profile of v4, /device:TPU:0, one launch (start us, length us, event | category | flops | bytes accessed | tf_op | source)
XLA Modules:
  0.0 40.3 jit_solution(2691628571789517944)
XLA Ops:
  0.0 39.7 %shard_map.64 = bf16[4,8,8,256]{3,2,1,0:T(8,128)(2,1)S(1)} custom-call(bf16[8,16,16,128]{3,2,1,0:T(8,128)(2,1)} %v_h.1, bf16[9,384,128]{2,1,0:T(8,128)(2,1)} %bitcast.9, bf16[27,128,256]{2,1,0:T(8,128)(2,1)} %bitcast.7, bf16[27,256,128]{2,1,0:T(8,128)(2,1)} %bitcast.8, bf16[27,512,128]{2,1,0:T(8,128)(2,1)} %bitcast.6, bf16[27,768,256]{2,1,0:T(8,128)(2,1)} %bitcast.5), custom_call_target="tpu_custom_call" | custom-call | tf_op jit(solution)/shard_map/pallas_call | solution.py:616
  39.7 0.7 %copy.8 = bf16[4,8,8,256]{3,2,1,0:T(8,128)(2,1)} copy(bf16[4,8,8,256]{3,2,1,0:T(8,128)(2,1)S(1)} %shard_map.64) | data formatting | bytes 262144

commit v5 on v4

--- a/solution.py
+++ b/solution.py
@@ -18,6 +18,15 @@
     if d < 0:
         return pl.ds(pad, 1), pl.ds(n + 1, 1)
     return pl.ds(pad + n - 1, 1), pl.ds(0, 1)
+
+
+def halves(pairs, refs):
+    for i, ref in enumerate(refs):
+        total = None
+        for lhs, rhs in pairs[i::2]:
+            part = jnp.dot(lhs, rhs, preferred_element_type=F32)
+            total = part if total is None else total + part
+        ref[...] = total
 
 
 def kernel(
@@ -28,7 +37,7 @@
     p1, f1, g1, gs, e1, a1, rz, t1,
     p2, f2, g2, e2, o2,
     p3, f3, g3, e3, o3, acc,
-    pk2, l2, m2, sel2, selm, q2, b2, pk3, l3, q3, b3, pk4, l4, up, sums, deeps, thirds,
+    pk2, l2, m2, sel2, selm, q2, b2, pk3, l3, q3, b3, pk4, l4, up, sums, deeps, brims, thirds, ends,
     s1, r1, s2, r2, s3, r3, s4, r4, s5, r5, s6, r6,
 ):
     gxn, gyn = dims
@@ -89,6 +98,7 @@
                     )
 
                 on(exists(0, dy), signal)
+    loads[0].start()
     lines = 1 + (gy > 0).astype(jnp.int32) + (gy < gyn - 1).astype(jnp.int32)
 
     def edge(block):
@@ -104,7 +114,7 @@
         for y in (0, ref.shape[1] - 1):
             ref[:, y] = jnp.zeros(ref.shape[:1] + ref.shape[2:], BF16)
     fetch.wait()
-    for load in loads:
+    for load in loads[1:]:
         load.start()
     for x in range(nx):
         f1[x] = edge(p1[x + 1, 1 : ny + 1].astype(F32))
@@ -133,6 +143,7 @@
     def drain(ref, sem):
         pltpu.make_async_copy(ref, ref, sem).wait()
 
+    stage = pl.when(gx < gxn)
     late = []
 
     def neighbours(src, pad, face, rim, side, nx, ny, ss, rs):
@@ -215,23 +226,26 @@
     for x in range(nx + 2):
         for y in range(ny + 2):
             gs[x, y : y + 1] = g1[x, y]
-    lhs = [gs[ox : ox + nx, oy : oy + ny].reshape(nx * ny, c0).astype(BF16) for ox in range(3) for oy in range(3)]
-    rz[...] = jnp.dot(jnp.concatenate(lhs, axis=1), wz[...], preferred_element_type=F32)
-    for x, ox, lane in ((0, 0, 0), (nx + 1, 2, c0)):
-        widen((x, pl.ds(1, ny)), p1[x, 1 : ny + 1])
-        lhs = [e1[x, oy : oy + ny].reshape(ny * nz, k0) for oy in range(3)]
-        rhs = wf[ox * 3 : ox * 3 + 3].reshape(3 * k0, c0)
-        part = jnp.dot(jnp.concatenate(lhs, axis=1), rhs, preferred_element_type=F32)
-        at = (0 if ox == 0 else nx // 2 - 1, slice(None), pl.ds(lane, c0))
-        a1[at] = a1[at] + part
-    for y, oy in ((0, 0), (ny + 1, 2)):
-        widen((pl.ds(0, nx + 2), y), p1[:, y])
-        lhs = [e1[ox : ox + nx, y].reshape(nx * nz, k0) for ox in range(3)]
-        rhs = jnp.concatenate([wf[ox * 3 + oy] for ox in range(3)], axis=0)
-        part = jnp.dot(jnp.concatenate(lhs, axis=1), rhs, preferred_element_type=F32).reshape(nx, nz, c0)
-        for x in range(nx):
-            at = (x // 2, pl.ds((0 if oy == 0 else ny - 1) * nz, nz), pl.ds(x % 2 * c0, c0))
-            a1[at] = a1[at] + part[x]
+    @stage
+    def _():
+        lhs = [gs[ox : ox + nx, oy : oy + ny].reshape(nx * ny, c0).astype(BF16) for ox in range(3) for oy in range(3)]
+        rz[...] = jnp.dot(jnp.concatenate(lhs, axis=1), wz[...], preferred_element_type=F32)
+        for x, ox, lane in ((0, 0, 0), (nx + 1, 2, c0)):
+            widen((x, pl.ds(1, ny)), p1[x, 1 : ny + 1])
+            lhs = [e1[x, oy : oy + ny].reshape(ny * nz, k0) for oy in range(3)]
+            rhs = wf[ox * 3 : ox * 3 + 3].reshape(3 * k0, c0)
+            part = jnp.dot(jnp.concatenate(lhs, axis=1), rhs, preferred_element_type=F32)
+            at = (0 if ox == 0 else nx // 2 - 1, slice(None), pl.ds(lane, c0))
+            a1[at] = a1[at] + part
+        for y, oy in ((0, 0), (ny + 1, 2)):
+            widen((pl.ds(0, nx + 2), y), p1[:, y])
+            lhs = [e1[ox : ox + nx, y].reshape(nx * nz, k0) for ox in range(3)]
+            rhs = jnp.concatenate([wf[ox * 3 + oy] for ox in range(3)], axis=0)
+            part = jnp.dot(jnp.concatenate(lhs, axis=1), rhs, preferred_element_type=F32).reshape(nx, nz, c0)
+            for x in range(nx):
+                at = (x // 2, pl.ds((0 if oy == 0 else ny - 1) * nz, nz), pl.ds(x % 2 * c0, c0))
+                a1[at] = a1[at] + part[x]
+
     tile = 8
     last = lax.broadcasted_iota(jnp.int32, (tile, c0), 0) == (tile - 1) * oz
     for x in range(nx):
@@ -269,18 +283,16 @@
             below, above = shifted(block, g[x])
             for k, part in enumerate((below, block, above)):
                 pack(even, odd, x, part, k * c)
-        sums[...] = jnp.zeros_like(sums)
-
-        @pl.loop(0, 3)
-        def _(ox):
-            total = sums[...]
-            for oy, (r, lo) in enumerate(((even, 0), (odd, 0), (even, 1))):
-                lhs = r[pl.ds(ox, hx), lo : lo + hy // 2].reshape(rows, 3 * c)
-                rhs = w[pl.ds(ox * 9 + oy * 3, 3)].reshape(3 * c, w.shape[2])
-                total = total + jnp.dot(lhs, rhs, preferred_element_type=F32)
-            sums[...] = total
-
-        return sums[...]
+        @stage
+        def _():
+            pairs = []
+            for ox in range(3):
+                for oy, (r, lo) in enumerate(((even, 0), (odd, 0), (even, 1))):
+                    rhs = w[ox * 9 + oy * 3 : ox * 9 + oy * 3 + 3].reshape(3 * c, w.shape[2])
+                    pairs.append((r[ox : ox + hx, lo : lo + hy // 2].reshape(rows, 3 * c), rhs))
+            halves(pairs, (sums.at[0], sums.at[1]))
+
+        return sums[0] + sums[1]
 
     loads[1].wait()
     c1 = wh.shape[2]
@@ -436,36 +448,38 @@
         return jnp.concatenate(lhs, axis=1)
 
     def bottom_own(pair, w):
-        k = 3 * w.shape[1]
-        deeps[...] = jnp.zeros_like(deeps)
-
-        @pl.loop(0, 3)
-        def _(ox):
-            lhs = window(pair, ox, 1, cy)
-            rhs = [w[pl.ds(ox * 9 + oy * 3, 3)].reshape(k, fo) for oy in range(3)]
-            if fo % 128 == 0:
-                total = jnp.dot(lhs, jnp.concatenate(rhs, axis=1), preferred_element_type=F32)
-                total = [total[:, oy * fo : (oy + 1) * fo] for oy in range(3)]
-            else:
-                total = [jnp.dot(lhs, r, preferred_element_type=F32) for r in rhs]
-            for oy in range(3):
-                deeps[oy] = deeps[oy] + total[oy]
+        @stage
+        def _():
+            k = 3 * w.shape[1]
+            pairs = []
+            for ox in range(3):
+                lhs = window(pair, ox, 1, cy)
+                rhs = [w[ox * 9 + oy * 3 : ox * 9 + oy * 3 + 3].reshape(k, fo) for oy in range(3)]
+                rhs = jnp.concatenate(rhs, axis=1)
+                pairs += [(lhs[:, : k // 2], rhs[: k // 2]), (lhs[:, k // 2 :], rhs[k // 2 :])]
+            halves(pairs, (deeps.at[0], deeps.at[1]))
 
     def bottom_rim(pair, w):
         k = 3 * w.shape[1]
         size = cz * ax
-        ends = []
-        for row, oy in ((0, 0), (cy + 1, 2)):
-            total = jnp.zeros((size, fo), F32)
-            for ox in range(3):
-                rhs = w[(ox * 3 + oy) * 3 : (ox * 3 + oy) * 3 + 3].reshape(k, fo)
-                total = total + jnp.dot(window(pair, ox, row, 1), rhs, preferred_element_type=F32)
-            ends.append(total)
+        @stage
+        def _():
+            for side, (row, oy) in enumerate(((0, 0), (cy + 1, 2))):
+                total = jnp.zeros((size, fo), F32)
+                for ox in range(3):
+                    rhs = w[(ox * 3 + oy) * 3 : (ox * 3 + oy) * 3 + 3].reshape(k, fo)
+                    total = total + jnp.dot(window(pair, ox, row, 1), rhs, preferred_element_type=F32)
+                brims[side] = total
+
+        def own(oy, y):
+            at = (pl.ds(y * size, size), pl.ds(oy * fo, fo))
+            return deeps[(0, *at)] + deeps[(1, *at)]
+
         lines = []
         for y in range(cy):
-            before = deeps[0, (y - 1) * size : y * size] if y > 0 else ends[0]
-            after = deeps[2, (y + 1) * size : (y + 2) * size] if y < cy - 1 else ends[1]
-            lines.append(deeps[1, y * size : (y + 1) * size] + before + after)
+            before = own(0, y - 1) if y > 0 else brims[0]
+            after = own(2, y + 1) if y < cy - 1 else brims[1]
+            lines.append(own(1, y) + before + after)
         return jnp.maximum(jnp.concatenate(lines, axis=0), 0.0).reshape(cy, cz, ax, fo).astype(BF16)
 
     main4(r4)
@@ -526,49 +540,58 @@
     main6, rim6 = leave(column_exchange(narrow_copy, *parts_of(l4)), s6)
     size = hx * hz
 
-    def enlarge(y):
-        field = jnp.concatenate([l4[g, y].astype(F32) for g in range(gxn)], axis=-1)
-        field = field.reshape((cz + 4) * near, c2).astype(BF16)
-        field = jnp.dot(pick, field, preferred_element_type=F32).astype(BF16)
-        for k in range(3):
-            at = pl.ds(k * c2, c2)
-            part = field[k * (size + 2 * hz) : (k + 1) * (size + 2 * hz)]
-            up[0, y, :, :, at] = part[:size].reshape(hx // 2, 2 * hz, c2)
-            up[2, y, :, :, at] = part[2 * hz :].reshape(hx // 2, 2 * hz, c2)
-            part = field[3 * (size + 2 * hz) + k * size : 3 * (size + 2 * hz) + (k + 1) * size]
-            up[1, y, :, :, at] = part.reshape(hx // 2, 2 * hz, c2)
-
-    thirds[...] = jnp.zeros_like(thirds)
+    def enlarge(ys):
+        fields = [l4[g, y].astype(F32).reshape((cz + 4) * near, fo) for y in ys for g in range(gxn)]
+        fields = jnp.concatenate(fields, axis=-1).astype(BF16)
+        fields = jnp.dot(pick, fields, preferred_element_type=F32).astype(BF16)
+        for i, y in enumerate(ys):
+            field = fields[:, i * c2 : (i + 1) * c2]
+            for k in range(3):
+                at = pl.ds(k * c2, c2)
+                part = field[k * (size + 2 * hz) : (k + 1) * (size + 2 * hz)]
+                up[0, y, :, :, at] = part[:size].reshape(hx // 2, 2 * hz, c2)
+                up[2, y, :, :, at] = part[2 * hz :].reshape(hx // 2, 2 * hz, c2)
+                part = field[3 * (size + 2 * hz) + k * size : 3 * (size + 2 * hz) + (k + 1) * size]
+                up[1, y, :, :, at] = part.reshape(hx // 2, 2 * hz, c2)
+
     main6(r6)
-    for y in range(1, cy + 1):
-        enlarge(y)
+    enlarge(range(1, cy + 1))
     loads[5].wait()
 
-    @pl.loop(0, 3)
-    def _(ox):
-        lhs = up[ox, 1 : cy + 1].reshape(cy * size, 3 * c2)
+    @stage
+    def _():
         for oy in range(3):
-            rhs = wuu[pl.ds(ox * 9 + oy * 3, 3)].reshape(3 * c2, c1)
-            thirds[oy] = thirds[oy] + jnp.dot(lhs, rhs, preferred_element_type=F32)
+            pairs = []
+            for ox in range(3):
+                for k in range(3):
+                    lhs = up[ox, 1 : cy + 1, :, :, pl.ds(k * c2, c2)].reshape(cy * size, c2)
+                    pairs.append((lhs, wuu[ox * 9 + oy * 3 + k]))
+            halves(pairs, (thirds.at[0, oy], thirds.at[1, oy]))
 
     for y in range(hy):
         line = acc[:, y]
         for oy in range(3):
             at = (y + oy + 1) // 2 - 1
             if 0 <= at < cy:
-                line = line + thirds[oy, at * size : (at + 1) * size].reshape(hx, hz, c1)
+                part = thirds[0, oy, at * size : (at + 1) * size] + thirds[1, oy, at * size : (at + 1) * size]
+                line = line + part.reshape(hx, hz, c1)
         if 0 < y < hy - 1:
             out[:, y] = line.astype(BF16)
         else:
             acc[:, y] = line
     rim6(r6)
-    for row, oy, y in ((0, 0, 0), (cy + 1, 2, hy - 1)):
-        enlarge(row)
-        total = jnp.zeros((size, c1), F32)
-        for ox in range(3):
-            rhs = wuu[(ox * 3 + oy) * 3 : (ox * 3 + oy) * 3 + 3].reshape(3 * c2, c1)
-            total = total + jnp.dot(up[ox, row].reshape(size, 3 * c2), rhs, preferred_element_type=F32)
-        out[:, y] = (acc[:, y] + total.reshape(hx, hz, c1)).astype(BF16)
+    enlarge((0, cy + 1))
+    @stage
+    def _():
+        for side, (row, oy) in enumerate(((0, 0), (cy + 1, 2))):
+            total = jnp.zeros((size, c1), F32)
+            for ox in range(3):
+                rhs = wuu[(ox * 3 + oy) * 3 : (ox * 3 + oy) * 3 + 3].reshape(3 * c2, c1)
+                total = total + jnp.dot(up[ox, row].reshape(size, 3 * c2), rhs, preferred_element_type=F32)
+            ends[side] = total
+
+    for side, y in enumerate((0, hy - 1)):
+        out[:, y] = (acc[:, y] + ends[side].reshape(hx, hz, c1)).astype(BF16)
 
     for fn in late:
         fn()
@@ -610,7 +633,8 @@
         vm((3, cy + 2, cz // 2 + 1, 2 * ax, c2), BF16), vm((3, cy + 2, cz // 2, 2 * ax, c2), BF16),
         vm((gxn, cy, cz // 2, 2 * (cx + 2), fo), BF16), vm((gxn, cy + 2, cz // 2 + 2, 2 * (cx + 2), fo), BF16),
         vm((3, cy + 2, hx // 2, 2 * hz, 3 * c2), BF16),
-        vm((hx * hy * hz, c1), F32), vm((3, cy * cz * ax, fo), F32), vm((3, cy * hx * hz, c1), F32),
+        vm((2, hx * hy * hz, c1), F32), vm((2, cy * cz * ax, 3 * fo), F32), vm((2, cz * ax, fo), F32),
+        vm((2, 3, cy * hx * hz, c1), F32), vm((2, hx * hz, c1), F32),
     ]
     scratch += [dma((3,))] * 12
     return pl.pallas_call(

time: 40.5 us -> 39.6 us (0.978)
  Pallas kernels: 39.7 us -> 38.8 us
    pallas_call x1, Pallas kernels: 39.7 us -> 38.8 us  [on_device(): pl.pallas_call(functools.partial(kernel, dims), out_shape=jax.ShapeDtypeS...]
where the time goes in v5:
time: 39.6 us; the launch traced here: 39.4 us
  Pallas kernels  38.8 us (98%)
  local copies, waits for them, and re-layouts  0.66 us (2%)
    pallas_call x1, Pallas kernels, on_device(): pl.pallas_call(functools.partial(kernel, dims), out_shape=jax.ShapeDtypeS...  38.8 us

profile of v5, /device:TPU:0, one launch (start us, length us, event | category | flops | bytes accessed | tf_op | source)
XLA Modules:
  0.0 39.4 jit_solution(11362769233454687902)
XLA Ops:
  0.0 38.8 %shard_map.64 = bf16[4,8,8,256]{3,2,1,0:T(8,128)(2,1)S(1)} custom-call(bf16[8,16,16,128]{3,2,1,0:T(8,128)(2,1)} %v_h.1, bf16[9,384,128]{2,1,0:T(8,128)(2,1)} %bitcast.9, bf16[27,128,256]{2,1,0:T(8,128)(2,1)} %bitcast.7, bf16[27,256,128]{2,1,0:T(8,128)(2,1)} %bitcast.8, bf16[27,512,128]{2,1,0:T(8,128)(2,1)} %bitcast.6, bf16[27,768,256]{2,1,0:T(8,128)(2,1)} %bitcast.5), custom_call_target="tpu_custom_call" | custom-call | tf_op jit(solution)/shard_map/pallas_call | solution.py:640
  38.8 0.7 %copy.8 = bf16[4,8,8,256]{3,2,1,0:T(8,128)(2,1)} copy(bf16[4,8,8,256]{3,2,1,0:T(8,128)(2,1)S(1)} %shard_map.64) | data formatting | bytes 262144

commit v6 on v5

--- a/solution.py
+++ b/solution.py
@@ -144,6 +144,13 @@
         pltpu.make_async_copy(ref, ref, sem).wait()
 
     stage = pl.when(gx < gxn)
+    short = jnp.minimum(gx, gxn - 1 - gx)
+    farthest = []
+    for i in range(gxn - 1, 0, -1):
+        paired = gx + ((i + 1) // 2 if i % 2 else -(i // 2))
+        rest = jnp.where(gx < gxn - 1 - gx, gx + (i - short), gx - (i - short))
+        farthest.append(jnp.where(i <= 2 * short, paired, rest))
+
     late = []
 
     def neighbours(src, pad, face, rim, side, nx, ny, ss, rs):
@@ -212,15 +219,22 @@
     for tap in range(9):
         wz[pl.ds(tap * c0, c0)] = wf[tap, pl.ds(pl.multiple_of(2 * oz * c0, c0), c0)]
 
-    @pl.loop(0, nx // 2)
-    def _(x):
-        total = jnp.zeros((ny * nz, 2 * c0), F32)
+    group1 = 2 if nx % 4 == 0 else 1
+
+    @pl.loop(0, nx // (2 * group1))
+    def _(step):
+        total = jnp.zeros((group1 * ny * nz, 2 * c0), F32)
         for oy in range(3):
             for half in range(2):
-                lhs = [e1[2 * x + 2 * half + i, oy : oy + ny].reshape(ny * nz, k0) for i in range(2)]
+                lhs = []
+                for i in range(2):
+                    planes = [2 * (step * group1 + n) + 2 * half + i for n in range(group1)]
+                    planes = [e1[x, oy : oy + ny].reshape(ny * nz, k0) for x in planes]
+                    lhs.append(jnp.concatenate(planes, axis=0))
                 rhs = wt[oy, 2 * half * k0 : 2 * (half + 1) * k0]
                 total = total + jnp.dot(jnp.concatenate(lhs, axis=1), rhs, preferred_element_type=F32)
-        a1[x] = total
+        for n in range(group1):
+            a1[step * group1 + n] = total[n * ny * nz : (n + 1) * ny * nz]
 
     arrived()
     for x in range(nx + 2):
@@ -299,7 +313,6 @@
     total = conv(e2, o2, p2, g2, wh)
     skip = rounded(jnp.maximum(total, 0.0)).reshape(hx, hy, hz, c1)
     p3[1 : hx + 1, 1 : hy + 1] = skip.astype(BF16)
-    f3[...] = edge(skip)
 
     cx, cy, cz = hx // 2, hy // 2, hz // 2
     ax = gxn * cx
@@ -368,15 +381,11 @@
         return make
 
     def column_exchange(choose, main, rim):
-        far = list(range(1, gxn))
-        for s, dy, z in (
-            [(s, 0, 0) for s in far]
-            + [(s, 0, 1) for s in far + [0]]
-            + [(s, dy, 0) for s in far + [0] for dy in (-1, 1)]
-            + [(s, dy, 1) for s in far + [0] for dy in (-1, 1)]
-        ):
-            k = 2 if dy else (0 if s else 1)
-            on(exists(0, dy), choose(k, dy, z)(gx, lax.rem(gx + s, gxn)).start)
+        order = [(there, 0, z, 0) for there in farthest for z in (0, 1)]
+        order += [(gx, 0, 1, 1)]
+        order += [(there, dy, z, 2) for there in farthest + [gx] for z in (0, 1) for dy in (-1, 1)]
+        for there, dy, z, k in order:
+            on(exists(0, dy), choose(k, dy, z)(gx, there).start)
 
         def first(which):
             for k, ref in enumerate(main):
@@ -399,6 +408,8 @@
     main4, rim4 = leave(
         column_exchange(coarse_copy, (l2.at[0 : gxn - 1], l2.at[0, 0:1]), lambda b: m2.at[0:gxn, 0 : 2 * b]), s4
     )
+    for x in range(hx):
+        f3[x] = edge(p3[x + 1, 1 : hy + 1].astype(F32))
 
     def one_hot(ref, at, slots):
         width = gxn * slots * group
@@ -483,7 +494,6 @@
         return jnp.maximum(jnp.concatenate(lines, axis=0), 0.0).reshape(cy, cz, ax, fo).astype(BF16)
 
     main4(r4)
-    skip_arrived = neighbours(p3, 1, f3, p3, g3, hx, hy, s3, r3)
     spread(q2, b2, gathered(sel2, l2), 1)
     loads[2].wait()
     bottom_own((q2, b2), w1)
@@ -496,11 +506,7 @@
     l3[gx, 1 : cy + 1, 1 : cz + 1] = first
     main5, rim5 = leave(column_exchange(deep_copy(pk3, l3, s5, r5), *parts_of(l3)), s5)
 
-    skip_arrived()
-    loads[4].wait()
-    total = conv(e3, o3, p3, g3, wus)
-    acc[...] = total.reshape(hx, hy, hz, c1)
-
+    skip_arrived = neighbours(p3, 1, f3, p3, g3, hx, hy, s3, r3)
     near = cx + 2
     wide = gxn * cz * near
     lane = lax.broadcasted_iota(jnp.int32, (wide, cz * ax), 1)
@@ -554,44 +560,42 @@
                 part = field[3 * (size + 2 * hz) + k * size : 3 * (size + 2 * hz) + (k + 1) * size]
                 up[1, y, :, :, at] = part.reshape(hx // 2, 2 * hz, c2)
 
+    skip_arrived()
+    loads[4].wait()
+    total = conv(e3, o3, p3, g3, wus)
+    acc[...] = total.reshape(hx, hy, hz, c1)
+
     main6(r6)
     enlarge(range(1, cy + 1))
     loads[5].wait()
 
     @stage
     def _():
-        for oy in range(3):
-            pairs = []
-            for ox in range(3):
-                for k in range(3):
-                    lhs = up[ox, 1 : cy + 1, :, :, pl.ds(k * c2, c2)].reshape(cy * size, c2)
-                    pairs.append((lhs, wuu[ox * 9 + oy * 3 + k]))
-            halves(pairs, (thirds.at[0, oy], thirds.at[1, oy]))
-
-    for y in range(hy):
-        line = acc[:, y]
-        for oy in range(3):
-            at = (y + oy + 1) // 2 - 1
-            if 0 <= at < cy:
-                part = thirds[0, oy, at * size : (at + 1) * size] + thirds[1, oy, at * size : (at + 1) * size]
-                line = line + part.reshape(hx, hz, c1)
-        if 0 < y < hy - 1:
-            out[:, y] = line.astype(BF16)
-        else:
-            acc[:, y] = line
+        pairs = []
+        for ox in range(3):
+            for k in range(3):
+                lhs = up[ox, 1 : cy + 1, :, :, pl.ds(k * c2, c2)].reshape(cy * size, c2)
+                pairs.append((lhs, wuu[ox * 9 + 3 + k]))
+        halves(pairs, (thirds.at[0], thirds.at[1]))
+
     rim6(r6)
     enlarge((0, cy + 1))
+
     @stage
     def _():
-        for side, (row, oy) in enumerate(((0, 0), (cy + 1, 2))):
-            total = jnp.zeros((size, c1), F32)
+        for side, oy in enumerate((0, 2)):
+            total = jnp.zeros(((cy + 1) * size, c1), F32)
             for ox in range(3):
+                lhs = up[ox, side : side + cy + 1].reshape((cy + 1) * size, 3 * c2)
                 rhs = wuu[(ox * 3 + oy) * 3 : (ox * 3 + oy) * 3 + 3].reshape(3 * c2, c1)
-                total = total + jnp.dot(up[ox, row].reshape(size, 3 * c2), rhs, preferred_element_type=F32)
+                total = total + jnp.dot(lhs, rhs, preferred_element_type=F32)
             ends[side] = total
 
-    for side, y in enumerate((0, hy - 1)):
-        out[:, y] = (acc[:, y] + ends[side].reshape(hx, hz, c1)).astype(BF16)
+    for y in range(hy):
+        low, mid, high = (y + 1) // 2, (y + 2) // 2 - 1, (y + 3) // 2 - 1
+        total = ends[0, low * size : (low + 1) * size] + ends[1, high * size : (high + 1) * size]
+        total = total + thirds[0, mid * size : (mid + 1) * size] + thirds[1, mid * size : (mid + 1) * size]
+        out[:, y] = (acc[:, y] + total.reshape(hx, hz, c1)).astype(BF16)
 
     for fn in late:
         fn()
@@ -634,7 +638,7 @@
         vm((gxn, cy, cz // 2, 2 * (cx + 2), fo), BF16), vm((gxn, cy + 2, cz // 2 + 2, 2 * (cx + 2), fo), BF16),
         vm((3, cy + 2, hx // 2, 2 * hz, 3 * c2), BF16),
         vm((2, hx * hy * hz, c1), F32), vm((2, cy * cz * ax, 3 * fo), F32), vm((2, cz * ax, fo), F32),
-        vm((2, 3, cy * hx * hz, c1), F32), vm((2, hx * hz, c1), F32),
+        vm((2, cy * hx * hz, c1), F32), vm((2, (cy + 1) * hx * hz, c1), F32),
     ]
     scratch += [dma((3,))] * 12
     return pl.pallas_call(

time: 39.6 us -> 38.6 us (0.975)
  Pallas kernels: 38.8 us -> 37.8 us
    pallas_call x1, Pallas kernels: 38.8 us -> 37.8 us  [on_device(): pl.pallas_call(functools.partial(kernel, dims), out_shape=jax.ShapeDtypeS...]
where the time goes in v6:
time: 38.6 us; the launch traced here: 38.5 us
  Pallas kernels  37.8 us (98%)
  local copies, waits for them, and re-layouts  0.66 us (2%)
    pallas_call x1, Pallas kernels, on_device(): pl.pallas_call(functools.partial(kernel, dims), out_shape=jax.ShapeDtypeS...  37.8 us

profile of v6, /device:TPU:0, one launch (start us, length us, event | category | flops | bytes accessed | tf_op | source)
XLA Modules:
  0.0 38.5 jit_solution(6450752258594343782)
XLA Ops:
  0.0 37.8 %shard_map.64 = bf16[4,8,8,256]{3,2,1,0:T(8,128)(2,1)S(1)} custom-call(bf16[8,16,16,128]{3,2,1,0:T(8,128)(2,1)} %v_h.1, bf16[9,384,128]{2,1,0:T(8,128)(2,1)} %bitcast.9, bf16[27,128,256]{2,1,0:T(8,128)(2,1)} %bitcast.7, bf16[27,256,128]{2,1,0:T(8,128)(2,1)} %bitcast.8, bf16[27,512,128]{2,1,0:T(8,128)(2,1)} %bitcast.6, bf16[27,768,256]{2,1,0:T(8,128)(2,1)} %bitcast.5), custom_call_target="tpu_custom_call" | custom-call | tf_op jit(solution)/shard_map/pallas_call | solution.py:644
  37.8 0.7 %copy.8 = bf16[4,8,8,256]{3,2,1,0:T(8,128)(2,1)} copy(bf16[4,8,8,256]{3,2,1,0:T(8,128)(2,1)S(1)} %shard_map.64) | data formatting | bytes 262144

commit v7 on v6

--- a/solution.py
+++ b/solution.py
@@ -33,7 +33,7 @@
     dims,
     v_h, wf_h, wh_h, w1_h, w2_h, wu_h,
     out,
-    wf, wh, w1, w2, wus, wuu, wsem, vsem, wt, wz,
+    wh, w1, w2, wus, wuu, wsem, vsem, fsem, wt, wz,
     p1, f1, g1, gs, e1, a1, rz, t1,
     p2, f2, g2, e2, o2,
     p3, f3, g3, e3, o3, acc,
@@ -51,7 +51,7 @@
     loads = [
         pltpu.make_async_copy(src, dst, wsem.at[i])
         for i, (src, dst) in enumerate((
-            (wf_h, wf), (wh_h, wh), (w1_h, w1), (w2_h, w2), (wu_h.at[:, c2:], wus), (wu_h.at[:, :c2], wuu),
+            (wh_h, wh), (w1_h, w1), (w2_h, w2), (wu_h.at[:, c2:], wus), (wu_h.at[:, :c2], wuu),
         ))
     ]
 
@@ -79,8 +79,11 @@
         p1[x] = jnp.zeros(p1.shape[1:], BF16)
     for y in (0, ny + 1):
         p1[1 : nx + 1, y] = jnp.zeros((nx, nz, c0), BF16)
-    for ref in (g1, m2, l3, l4):
-        ref[...] = jnp.zeros(ref.shape, ref.dtype)
+    m2[...] = jnp.zeros_like(m2)
+    for x in (0, nx + 1):
+        g1[x] = jnp.zeros(g1.shape[1:], F32)
+    for y in (0, ny + 1):
+        g1[:, y] = jnp.zeros((nx + 2, 1, c0), F32)
 
     barrier = pltpu.get_barrier_semaphore()
     for s in range(gxn):
@@ -98,7 +101,11 @@
                     )
 
                 on(exists(0, dy), signal)
-    loads[0].start()
+    k0 = 3 * c0
+    for oy in range(3):
+        for first, lane in ((0, 0), (1, c0)):
+            dst = wt.at[oy, first : first + 3, :, lane : lane + c0]
+            pltpu.make_async_copy(wf_h.at[:, oy], dst, fsem).start()
     lines = 1 + (gy > 0).astype(jnp.int32) + (gy < gyn - 1).astype(jnp.int32)
 
     def edge(block):
@@ -113,8 +120,15 @@
             ref[x] = jnp.zeros(ref.shape[1:], BF16)
         for y in (0, ref.shape[1] - 1):
             ref[:, y] = jnp.zeros(ref.shape[:1] + ref.shape[2:], BF16)
+    for x in (0, nx + 1):
+        e1[x] = jnp.zeros(e1.shape[1:], BF16)
+    for y in (0, ny + 1):
+        e1[1 : nx + 1, y] = jnp.zeros((nx, nz, k0), BF16)
+    for oy in range(3):
+        wt[oy, 3, :, :c0] = jnp.zeros((k0, c0), BF16)
+        wt[oy, 0, :, c0:] = jnp.zeros((k0, c0), BF16)
     fetch.wait()
-    for load in loads[1:]:
+    for load in loads:
         load.start()
     for x in range(nx):
         f1[x] = edge(p1[x + 1, 1 : ny + 1].astype(F32))
@@ -154,17 +168,21 @@
     late = []
 
     def neighbours(src, pad, face, rim, side, nx, ny, ss, rs):
+        copies = []
         for dx, dy in STEPS:
             sx, tx = span(dx, nx, pad)
             sy, ty = span(dy, ny, pad)
             fx, _ = span(dx, nx, 0)
             fy, _ = span(dy, ny, 0)
-            copies = [send(face.at[fx, fy], side.at[tx, ty], ss.at[0], rs.at[0], gx + dx, gy + dy, oz)]
-            if (dx, dy) != (0, 0):
+            hops = abs(dx) + abs(dy)
+            to = (gx + dx, gy + dy)
+            copies.append((hops + 1, exists(dx, dy), send(face.at[fx, fy], side.at[tx, ty], ss.at[0], rs.at[0], *to, oz)))
+            if hops:
                 k = 1 if dx else 2
-                copies.append(send(src.at[sx, sy], rim.at[tx, ty], ss.at[k], rs.at[k], gx + dx, gy + dy, gz))
-            for copy in copies:
-                on(exists(dx, dy), copy.start)
+                copy = send(src.at[sx, sy], rim.at[tx, ty], ss.at[k], rs.at[k], *to, gz)
+                copies.append((hops, exists(dx, dy), copy))
+        for _, cond, copy in sorted(copies, key=lambda entry: -entry[0]):
+            on(cond, copy.start)
 
         def finish(sems):
             def both(a, b):
@@ -194,12 +212,6 @@
 
     arrived = neighbours(p1, 1, f1, p1, g1, nx, ny, s1, r1)
 
-    k0 = 3 * c0
-    for x in (0, nx + 1):
-        e1[x] = jnp.zeros(e1.shape[1:], BF16)
-    for y in (0, ny + 1):
-        e1[1 : nx + 1, y] = jnp.zeros((nx, nz, k0), BF16)
-
     def widen(at, block):
         block = block.astype(F32)
         below, above = shifted(block, None)
@@ -210,14 +222,7 @@
     def _(x):
         widen((x, pl.ds(1, ny)), p1[x, 1 : ny + 1])
 
-    loads[0].wait()
-    for oy in range(3):
-        for plane in range(4):
-            at = pl.ds(plane * k0, k0)
-            wt[oy, at, :c0] = wf[plane * 3 + oy] if plane < 3 else jnp.zeros((k0, c0), BF16)
-            wt[oy, at, c0:] = wf[(plane - 1) * 3 + oy] if plane > 0 else jnp.zeros((k0, c0), BF16)
-    for tap in range(9):
-        wz[pl.ds(tap * c0, c0)] = wf[tap, pl.ds(pl.multiple_of(2 * oz * c0, c0), c0)]
+    drain(wt.at[:, 0:3], fsem)
 
     group1 = 2 if nx % 4 == 0 else 1
 
@@ -231,11 +236,15 @@
                     planes = [2 * (step * group1 + n) + 2 * half + i for n in range(group1)]
                     planes = [e1[x, oy : oy + ny].reshape(ny * nz, k0) for x in planes]
                     lhs.append(jnp.concatenate(planes, axis=0))
-                rhs = wt[oy, 2 * half * k0 : 2 * (half + 1) * k0]
+                rhs = wt[oy, 2 * half : 2 * half + 2].reshape(2 * k0, 2 * c0)
                 total = total + jnp.dot(jnp.concatenate(lhs, axis=1), rhs, preferred_element_type=F32)
         for n in range(group1):
             a1[step * group1 + n] = total[n * ny * nz : (n + 1) * ny * nz]
 
+    for ox in range(3):
+        for oy in range(3):
+            tap = wt[oy, ox, pl.ds(pl.multiple_of(2 * oz * c0, c0), c0), :c0]
+            wz[(ox * 3 + oy) * c0 : (ox * 3 + oy + 1) * c0] = tap
     arrived()
     for x in range(nx + 2):
         for y in range(ny + 2):
@@ -247,14 +256,14 @@
         for x, ox, lane in ((0, 0, 0), (nx + 1, 2, c0)):
             widen((x, pl.ds(1, ny)), p1[x, 1 : ny + 1])
             lhs = [e1[x, oy : oy + ny].reshape(ny * nz, k0) for oy in range(3)]
-            rhs = wf[ox * 3 : ox * 3 + 3].reshape(3 * k0, c0)
+            rhs = jnp.concatenate([wt[oy, ox, :, :c0] for oy in range(3)], axis=0)
             part = jnp.dot(jnp.concatenate(lhs, axis=1), rhs, preferred_element_type=F32)
             at = (0 if ox == 0 else nx // 2 - 1, slice(None), pl.ds(lane, c0))
             a1[at] = a1[at] + part
         for y, oy in ((0, 0), (ny + 1, 2)):
             widen((pl.ds(0, nx + 2), y), p1[:, y])
             lhs = [e1[ox : ox + nx, y].reshape(nx * nz, k0) for ox in range(3)]
-            rhs = jnp.concatenate([wf[ox * 3 + oy] for ox in range(3)], axis=0)
+            rhs = jnp.concatenate([wt[oy, ox, :, :c0] for ox in range(3)], axis=0)
             part = jnp.dot(jnp.concatenate(lhs, axis=1), rhs, preferred_element_type=F32).reshape(nx, nz, c0)
             for x in range(nx):
                 at = (x // 2, pl.ds((0 if oy == 0 else ny - 1) * nz, nz), pl.ds(x % 2 * c0, c0))
@@ -281,6 +290,8 @@
         f2[x] = edge(small)
 
     arrived = neighbours(p2, 1, f2, p2, g2, hx, hy, s2, r2)
+    for ref in (l3, l4):
+        ref[...] = jnp.zeros(ref.shape, ref.dtype)
     arrived()
     rows = hx * hy * hz
 
@@ -308,7 +319,7 @@
 
         return sums[0] + sums[1]
 
-    loads[1].wait()
+    loads[0].wait()
     c1 = wh.shape[2]
     total = conv(e2, o2, p2, g2, wh)
     skip = rounded(jnp.maximum(total, 0.0)).reshape(hx, hy, hz, c1)
@@ -381,9 +392,9 @@
         return make
 
     def column_exchange(choose, main, rim):
-        order = [(there, 0, z, 0) for there in farthest for z in (0, 1)]
+        order = [(there, 0, z, 0) for there in farthest for z in (1, 0)]
         order += [(gx, 0, 1, 1)]
-        order += [(there, dy, z, 2) for there in farthest + [gx] for z in (0, 1) for dy in (-1, 1)]
+        order += [(there, dy, z, 2) for there in farthest + [gx] for z in (1, 0) for dy in (-1, 1)]
         for there, dy, z, k in order:
             on(exists(0, dy), choose(k, dy, z)(gx, there).start)
 
@@ -495,7 +506,7 @@
 
     main4(r4)
     spread(q2, b2, gathered(sel2, l2), 1)
-    loads[2].wait()
+    loads[1].wait()
     bottom_own((q2, b2), w1)
     rim4(r4)
     block = gathered(selm, m2)
@@ -532,7 +543,7 @@
 
     main5(r5)
     spread(q3, b3, joined(1, cy), 1)
-    loads[3].wait()
+    loads[2].wait()
     bottom_own((q3, b3), w2)
     rim5(r5)
     spread(q3, b3, joined(0, 1), 0)
@@ -561,13 +572,13 @@
                 up[1, y, :, :, at] = part.reshape(hx // 2, 2 * hz, c2)
 
     skip_arrived()
-    loads[4].wait()
+    loads[3].wait()
     total = conv(e3, o3, p3, g3, wus)
     acc[...] = total.reshape(hx, hy, hz, c1)
 
     main6(r6)
     enlarge(range(1, cy + 1))
-    loads[5].wait()
+    loads[4].wait()
 
     @stage
     def _():
@@ -610,7 +621,7 @@
     cx, cy, cz = hx // 2, hy // 2, hz // 2
     ax = gxn * cx
     weights = [
-        w_full.reshape(9, 3 * c0, c0),
+        w_full.reshape(3, 3, 3 * c0, c0),
         w_half.reshape(27, c0, c1),
         w_bottom_in.reshape(27, c1, fo),
         w_bottom_out.reshape(27, c2, fo),
@@ -618,9 +629,9 @@
     ]
     vm = pltpu.VMEM
     dma = pltpu.SemaphoreType.DMA
-    scratch = [vm(w.shape, BF16) for w in weights[:4]]
-    scratch += [vm((27, c1, c1), BF16), vm((27, c2, c1), BF16), dma((6,)), dma(())]
-    scratch += [vm((3, 12 * c0, 2 * c0), BF16), vm((9 * c0, c0), BF16)]
+    scratch = [vm(w.shape, BF16) for w in weights[1:4]]
+    scratch += [vm((27, c1, c1), BF16), vm((27, c2, c1), BF16), dma((5,)), dma(()), dma(())]
+    scratch += [vm((3, 4, 3 * c0, 2 * c0), BF16), vm((9 * c0, c0), BF16)]
     scratch += [
         vm((nx + 2, ny + 2, nz, c0), BF16), vm((nx, ny, 1, c0), F32), vm((nx + 2, ny + 2, 1, c0), F32),
         vm((nx + 2, ny + 2, c0), F32), vm((nx + 2, ny + 2, nz, 3 * c0), BF16), vm((hx, ny * nz, 2 * c0), F32),

time: 38.6 us -> 37.2 us (0.964)
  Pallas kernels: 37.8 us -> 36.4 us
    pallas_call x1, Pallas kernels: 37.8 us -> 36.4 us  [on_device(): pl.pallas_call(functools.partial(kernel, dims), out_shape=jax.ShapeDtypeS...]
where the time goes in v7:
time: 37.2 us; the launch traced here: 37.1 us
  Pallas kernels  36.4 us (98%)
  local copies, waits for them, and re-layouts  0.66 us (2%)
    pallas_call x1, Pallas kernels, on_device(): pl.pallas_call(functools.partial(kernel, dims), out_shape=jax.ShapeDtypeS...  36.4 us

profile of v7, /device:TPU:0, one launch (start us, length us, event | category | flops | bytes accessed | tf_op | source)
XLA Modules:
  0.0 37.1 jit_solution(9734595149775595950)
XLA Ops:
  0.0 36.4 %shard_map.64 = bf16[4,8,8,256]{3,2,1,0:T(8,128)(2,1)S(1)} custom-call(bf16[8,16,16,128]{3,2,1,0:T(8,128)(2,1)} %v_h.1, bf16[3,3,384,128]{3,2,1,0:T(8,128)(2,1)} %bitcast.9, bf16[27,128,256]{2,1,0:T(8,128)(2,1)} %bitcast.7, bf16[27,256,128]{2,1,0:T(8,128)(2,1)} %bitcast.8, bf16[27,512,128]{2,1,0:T(8,128)(2,1)} %bitcast.6, bf16[27,768,256]{2,1,0:T(8,128)(2,1)} %bitcast.5), custom_call_target="tpu_custom_call" | custom-call | tf_op jit(solution)/shard_map/pallas_call | solution.py:655
  36.4 0.7 %copy.8 = bf16[4,8,8,256]{3,2,1,0:T(8,128)(2,1)} copy(bf16[4,8,8,256]{3,2,1,0:T(8,128)(2,1)S(1)} %shard_map.64) | data formatting | bytes 262144

commit v8 on v7

--- a/solution.py
+++ b/solution.py
@@ -391,33 +391,59 @@
 
         return make
 
-    def column_exchange(choose, main, rim):
+    upper = lax.rem(gy, 2) == 1
+    lower = lax.rem(gy, 2) == 0
+    across = {-1: jnp.logical_and(lower, gy > 0), 1: jnp.logical_and(upper, gy < gyn - 1)}
+    within = {-1: upper, 1: lower}
+
+    def column_exchange(choose, main, rim, relay, carry, ss, rs):
         order = [(there, 0, z, 0) for there in farthest for z in (1, 0)]
         order += [(gx, 0, 1, 1)]
-        order += [(there, dy, z, 2) for there in farthest + [gx] for z in (1, 0) for dy in (-1, 1)]
         for there, dy, z, k in order:
-            on(exists(0, dy), choose(k, dy, z)(gx, there).start)
-
-        def first(which):
+            choose(k, dy, z)(gx, there).start()
+        for there in farthest + [gx]:
+            for z in (1, 0):
+                for dy in (-1, 1):
+                    on(across[dy], choose(2, dy, z)(gx, there).start)
+
+        def own(which):
             for k, ref in enumerate(main):
                 drain(ref, which.at[k])
 
-        def second(which):
-            by_y(lambda b: drain(rim(b), which.at[2]))
-
-        return first, second
-
-    def leave(waits, sems):
-        late.append(lambda: [wait(sems) for wait in waits])
-        return waits
+        def edges(which):
+            for dy in (-1, 1):
+                on(across[dy], lambda: drain(rim, which.at[2]))
+            drain(relay, which.at[3])
+
+        def arrive():
+            own(rs)
+            for dy in (-1, 1):
+                for src, dst in carry(dy):
+                    on(within[dy], send(src, dst, ss.at[3], rs.at[3], gx, gy + dy, gz).start)
+
+        def finish():
+            own(ss)
+            edges(ss)
+
+        late.append(finish)
+        return arrive, lambda: edges(rs)
 
     def parts_of(land):
         wz = land.shape[2] - 2
+
+        def carry(dy):
+            rows = (cy, 0) if dy > 0 else (1, cy + 1)
+            return [tuple(land.at[:, row] for row in rows)]
+
         main = (land.at[0 : gxn - 1, 0:cy, 0 : wz + 1], land.at[0, 0:cy, 0:1])
-        return main, lambda b: land.at[0:gxn, 0:b, 0 : wz + 1]
-
-    main4, rim4 = leave(
-        column_exchange(coarse_copy, (l2.at[0 : gxn - 1], l2.at[0, 0:1]), lambda b: m2.at[0:gxn, 0 : 2 * b]), s4
+        return main, land.at[0:gxn, 0:1, 0 : wz + 1], land.at[:, 0], carry
+
+    def carry_lines(dy):
+        pairs = ((cy - 1, 0), (cy, 2)) if dy > 0 else ((0, 1), (cy, 3))
+        return [(l2.at[:, line], m2.at[:, slot]) for line, slot in pairs]
+
+    main4, rim4 = column_exchange(
+        coarse_copy, (l2.at[0 : gxn - 1], l2.at[0, 0:1]), m2.at[:, 0:2], m2.at[:, 0:2], carry_lines, s4, r4
     )
     for x in range(hx):
         f3[x] = edge(p3[x + 1, 1 : hy + 1].astype(F32))
@@ -504,18 +530,18 @@
             lines.append(own(1, y) + before + after)
         return jnp.maximum(jnp.concatenate(lines, axis=0), 0.0).reshape(cy, cz, ax, fo).astype(BF16)
 
-    main4(r4)
+    main4()
     spread(q2, b2, gathered(sel2, l2), 1)
     loads[1].wait()
     bottom_own((q2, b2), w1)
-    rim4(r4)
+    rim4()
     block = gathered(selm, m2)
     spread(q2, b2, block[0:1], 0)
     spread(q2, b2, block[1:2], cy + 1)
     first = bottom_rim((q2, b2), w1)
     pk3[...] = first
     l3[gx, 1 : cy + 1, 1 : cz + 1] = first
-    main5, rim5 = leave(column_exchange(deep_copy(pk3, l3, s5, r5), *parts_of(l3)), s5)
+    main5, rim5 = column_exchange(deep_copy(pk3, l3, s5, r5), *parts_of(l3), s5, r5)
 
     skip_arrived = neighbours(p3, 1, f3, p3, g3, hx, hy, s3, r3)
     near = cx + 2
@@ -541,11 +567,11 @@
     def joined(row, n):
         return jnp.concatenate([l3[g, row : row + n].astype(F32) for g in range(gxn)], axis=-1)
 
-    main5(r5)
+    main5()
     spread(q3, b3, joined(1, cy), 1)
     loads[2].wait()
     bottom_own((q3, b3), w2)
-    rim5(r5)
+    rim5()
     spread(q3, b3, joined(0, 1), 0)
     spread(q3, b3, joined(cy + 1, 1), cy + 1)
     second = bottom_rim((q3, b3), w2)
@@ -554,7 +580,7 @@
         line = jnp.dot(share, line, preferred_element_type=F32)
         pk4[:, y] = line.reshape(gxn, cz // 2, 2 * near, fo).astype(BF16)
     l4[gx, 1 : cy + 1, 1 : cz // 2 + 1] = pk4[gx]
-    main6, rim6 = leave(column_exchange(narrow_copy, *parts_of(l4)), s6)
+    main6, rim6 = column_exchange(narrow_copy, *parts_of(l4), s6, r6)
     size = hx * hz
 
     def enlarge(ys):
@@ -576,7 +602,7 @@
     total = conv(e3, o3, p3, g3, wus)
     acc[...] = total.reshape(hx, hy, hz, c1)
 
-    main6(r6)
+    main6()
     enlarge(range(1, cy + 1))
     loads[4].wait()
 
@@ -589,7 +615,7 @@
                 pairs.append((lhs, wuu[ox * 9 + 3 + k]))
         halves(pairs, (thirds.at[0], thirds.at[1]))
 
-    rim6(r6)
+    rim6()
     enlarge((0, cy + 1))
 
     @stage
@@ -651,7 +677,7 @@
         vm((2, hx * hy * hz, c1), F32), vm((2, cy * cz * ax, 3 * fo), F32), vm((2, cz * ax, fo), F32),
         vm((2, cy * hx * hz, c1), F32), vm((2, (cy + 1) * hx * hz, c1), F32),
     ]
-    scratch += [dma((3,))] * 12
+    scratch += [dma((3,))] * 6 + [dma((4,))] * 6
     return pl.pallas_call(
         functools.partial(kernel, dims),
         out_shape=jax.ShapeDtypeStruct((hx, hy, hz, c1), BF16),
@@ -666,7 +692,7 @@
 
 def solution(mesh):
     dims = (mesh.shape["gx"], mesh.shape["gy"])
-    assert mesh.shape["gz"] == 2
+    assert mesh.shape["gz"] == 2 and mesh.shape["gy"] % 2 == 0
     return jax.shard_map(
         functools.partial(on_device, dims),
         mesh=mesh,

time: 37.2 us -> 36.8 us (0.989)
  Pallas kernels: 36.4 us -> 36 us
    pallas_call x1, Pallas kernels: 36.4 us -> 36 us  [on_device(): pl.pallas_call(functools.partial(kernel, dims), out_shape=jax.ShapeDtypeS...]
where the time goes in v8:
time: 36.8 us; the launch traced here: 36.7 us
  Pallas kernels  36 us (98%)
  local copies, waits for them, and re-layouts  0.66 us (2%)
    pallas_call x1, Pallas kernels, on_device(): pl.pallas_call(functools.partial(kernel, dims), out_shape=jax.ShapeDtypeS...  36 us

profile of v8, /device:TPU:0, one launch (start us, length us, event | category | flops | bytes accessed | tf_op | source)
XLA Modules:
  0.0 36.7 jit_solution(15449637007855807765)
XLA Ops:
  0.0 36.0 %shard_map.64 = bf16[4,8,8,256]{3,2,1,0:T(8,128)(2,1)S(1)} custom-call(bf16[8,16,16,128]{3,2,1,0:T(8,128)(2,1)} %v_h.1, bf16[3,3,384,128]{3,2,1,0:T(8,128)(2,1)} %bitcast.9, bf16[27,128,256]{2,1,0:T(8,128)(2,1)} %bitcast.7, bf16[27,256,128]{2,1,0:T(8,128)(2,1)} %bitcast.8, bf16[27,512,128]{2,1,0:T(8,128)(2,1)} %bitcast.6, bf16[27,768,256]{2,1,0:T(8,128)(2,1)} %bitcast.5), custom_call_target="tpu_custom_call" | custom-call | tf_op jit(solution)/shard_map/pallas_call | solution.py:681
  36.0 0.7 %copy.8 = bf16[4,8,8,256]{3,2,1,0:T(8,128)(2,1)} copy(bf16[4,8,8,256]{3,2,1,0:T(8,128)(2,1)S(1)} %shard_map.64) | data formatting | bytes 262144

commit v9 on v8

--- a/solution.py
+++ b/solution.py
@@ -110,8 +110,7 @@
 
     def edge(block):
         size = block.shape[-2]
-        rows = lax.broadcasted_iota(jnp.int32, block.shape, block.ndim - 2)
-        return jnp.sum(jnp.where(rows == (size - 1) * oz, block, 0.0), axis=block.ndim - 2, keepdims=True)
+        return jnp.where(oz == 0, block[..., 0:1, :], block[..., size - 1 : size, :])
 
     for ref in (g2, g3):
         ref[...] = jnp.zeros(ref.shape, ref.dtype)
@@ -397,7 +396,7 @@
     within = {-1: upper, 1: lower}
 
     def column_exchange(choose, main, rim, relay, carry, ss, rs):
-        order = [(there, 0, z, 0) for there in farthest for z in (1, 0)]
+        order = [(there, 0, z, 0) for z in (1, 0) for there in farthest]
         order += [(gx, 0, 1, 1)]
         for there, dy, z, k in order:
             choose(k, dy, z)(gx, there).start()

time: 36.8 us -> 36.5 us (level)
  no operation moved by 1% of the time
where the time goes in v9:
time: 36.5 us; the launch traced here: 36.4 us
  Pallas kernels  35.7 us (98%)
  local copies, waits for them, and re-layouts  0.66 us (2%)
    pallas_call x1, Pallas kernels, on_device(): pl.pallas_call(functools.partial(kernel, dims), out_shape=jax.ShapeDtypeS...  35.7 us

profile of v9, /device:TPU:0, one launch (start us, length us, event | category | flops | bytes accessed | tf_op | source)
XLA Modules:
  0.0 36.4 jit_solution(5509276082842095493)
XLA Ops:
  0.0 35.7 %shard_map.64 = bf16[4,8,8,256]{3,2,1,0:T(8,128)(2,1)S(1)} custom-call(bf16[8,16,16,128]{3,2,1,0:T(8,128)(2,1)} %v_h.1, bf16[3,3,384,128]{3,2,1,0:T(8,128)(2,1)} %bitcast.9, bf16[27,128,256]{2,1,0:T(8,128)(2,1)} %bitcast.7, bf16[27,256,128]{2,1,0:T(8,128)(2,1)} %bitcast.8, bf16[27,512,128]{2,1,0:T(8,128)(2,1)} %bitcast.6, bf16[27,768,256]{2,1,0:T(8,128)(2,1)} %bitcast.5), custom_call_target="tpu_custom_call" | custom-call | tf_op jit(solution)/shard_map/pallas_call | solution.py:680
  35.7 0.7 %copy.8 = bf16[4,8,8,256]{3,2,1,0:T(8,128)(2,1)} copy(bf16[4,8,8,256]{3,2,1,0:T(8,128)(2,1)S(1)} %shard_map.64) | data formatting | bytes 262144

commit v10 on v9

--- a/solution.py
+++ b/solution.py
@@ -37,7 +37,7 @@
     p1, f1, g1, gs, e1, a1, rz, t1,
     p2, f2, g2, e2, o2,
     p3, f3, g3, e3, o3, acc,
-    pk2, l2, m2, sel2, selm, q2, b2, pk3, l3, q3, b3, pk4, l4, up, sums, deeps, brims, thirds, ends,
+    pk2, l2, m2, sel2, selm, pick2, pickm, q2, b2, pk3, l3, q3, b3, pk4, l4, up, sums, deeps, brims, thirds, ends,
     s1, r1, s2, r2, s3, r3, s4, r4, s5, r5, s6, r6,
 ):
     gxn, gyn = dims
@@ -469,9 +469,13 @@
             else:
                 one_hot(selm, (rim_slot, z + 1), 4)
 
+    for wide, narrow in ((sel2, pick2), (selm, pickm)):
+        narrow[...] = wide[...].reshape(narrow.shape).astype(BF16)
+
     def gathered(ref, land):
-        n, width = ref.shape[0], ref.shape[-1]
-        select = ref[...].reshape(n * (cz + 2) * ax, width).astype(BF16)
+        width = ref.shape[-1]
+        n = ref.shape[0] // ((cz + 2) * ax)
+        select = ref[...]
         landed = land[...].astype(F32).reshape(width, c1).astype(BF16)
         return jnp.dot(select, landed, preferred_element_type=F32).reshape(n, cz + 2, ax, c1)
 
@@ -530,11 +534,11 @@
         return jnp.maximum(jnp.concatenate(lines, axis=0), 0.0).reshape(cy, cz, ax, fo).astype(BF16)
 
     main4()
-    spread(q2, b2, gathered(sel2, l2), 1)
+    spread(q2, b2, gathered(pick2, l2), 1)
     loads[1].wait()
     bottom_own((q2, b2), w1)
     rim4()
-    block = gathered(selm, m2)
+    block = gathered(pickm, m2)
     spread(q2, b2, block[0:1], 0)
     spread(q2, b2, block[1:2], cy + 1)
     first = bottom_rim((q2, b2), w1)
@@ -668,6 +672,7 @@
         vm((hx, hy, hz, c1), F32),
         vm((cy + 1, cz * cx, c1), BF16), vm((gxn, cy + 1, cz * cx, c1), BF16), vm((gxn, 4, cz * cx, c1), BF16),
         vm((cy, cz + 2, ax, gxn * (cy + 1) * cz * cx), F32), vm((2, cz + 2, ax, gxn * 4 * cz * cx), F32),
+        vm((cy * (cz + 2) * ax, gxn * (cy + 1) * cz * cx), BF16), vm((2 * (cz + 2) * ax, gxn * 4 * cz * cx), BF16),
         vm((3, cy + 2, cz // 2 + 1, 2 * ax, c1), BF16), vm((3, cy + 2, cz // 2, 2 * ax, c1), BF16),
         vm((cy, cz, ax, fo), BF16), vm((gxn, cy + 2, cz + 2, ax, fo), BF16),
         vm((3, cy + 2, cz // 2 + 1, 2 * ax, c2), BF16), vm((3, cy + 2, cz // 2, 2 * ax, c2), BF16),

time: 36.5 us -> 36.5 us (level)
  no operation moved by 1% of the time
where the time goes in v10:
time: 36.5 us; the launch traced here: 36.4 us
  Pallas kernels  35.7 us (98%)
  local copies, waits for them, and re-layouts  0.66 us (2%)
    pallas_call x1, Pallas kernels, on_device(): pl.pallas_call(functools.partial(kernel, dims), out_shape=jax.ShapeDtypeS...  35.7 us

profile of v10, /device:TPU:0, one launch (start us, length us, event | category | flops | bytes accessed | tf_op | source)
XLA Modules:
  0.0 36.4 jit_solution(13671858723205185514)
XLA Ops:
  0.0 35.7 %shard_map.64 = bf16[4,8,8,256]{3,2,1,0:T(8,128)(2,1)S(1)} custom-call(bf16[8,16,16,128]{3,2,1,0:T(8,128)(2,1)} %v_h.1, bf16[3,3,384,128]{3,2,1,0:T(8,128)(2,1)} %bitcast.9, bf16[27,128,256]{2,1,0:T(8,128)(2,1)} %bitcast.7, bf16[27,256,128]{2,1,0:T(8,128)(2,1)} %bitcast.8, bf16[27,512,128]{2,1,0:T(8,128)(2,1)} %bitcast.6, bf16[27,768,256]{2,1,0:T(8,128)(2,1)} %bitcast.5), custom_call_target="tpu_custom_call" | custom-call | tf_op jit(solution)/shard_map/pallas_call | solution.py:685
  35.7 0.7 %copy.8 = bf16[4,8,8,256]{3,2,1,0:T(8,128)(2,1)} copy(bf16[4,8,8,256]{3,2,1,0:T(8,128)(2,1)S(1)} %shard_map.64) | data formatting | bytes 262144
